TPU v7x, 16 devices: a whole 2x2x2 slice. The times are simulated.
16 devices in a mesh: col: 2 (over z), row: 8 (over y, x, core).
Axes of the slice: x: 2, y: 2, z: 2, core: 2. Of those that a mesh axis runs over, the one named last changes fastest.
Arguments:
- hyper_params: float32 [3], replicated
- w_in: float32 [4, 2048, 5120], P(None, 'row', 'col')
- x_in: bfloat16 [4, 512, 2048], P(None, None, 'row')
- dy_in: bfloat16 [4, 512, 5120], P(None, None, 'col')
- row_in: float32 [4, 2048], P(None, 'row')
- col_in: float32 [4, 5120], P(None, 'col')
- w_out: float32 [4, 5120, 2048], P(None, 'col', 'row')
- x_out: bfloat16 [4, 512, 5120], P(None, None, 'col')
- dy_out: bfloat16 [4, 512, 2048], P(None, None, 'row')
- row_out: float32 [4, 5120], P(None, 'col')
- col_out: float32 [4, 2048], P(None, 'row')
Outputs:
- output 1: float32 [4, 2048, 5120], P(None, 'row', 'col')
- output 2: float32 [4, 2048], P(None, 'row')
- output 3: float32 [4, 5120], P(None, 'col')
- output 4: float32 [4, 5120, 2048], P(None, 'col', 'row')
- output 5: float32 [4, 5120], P(None, 'col')
- output 6: float32 [4, 2048], P(None, 'row')
All inputs are finite; a program needn't handle non-finite values.
Results may differ from a plain program's by a relative error of at most 0.001.
Values are sent between devices in bfloat16 or wider.
A program may use at most 1 GiB of HBM per device.

v0:
```python
import jax
import jax.numpy as jnp
from jax import lax
from jax.sharding import PartitionSpec as P

EPS_ONE = 1e-30
EPS_TWO = 1e-3
BOTH_AXES = ('col', 'row')


def update_block(w_blk, x_blk, dy_blk, row_old, col_old, hyper_params, rows_axis, cols_axis, n_rows, n_cols):
    beta_two = hyper_params[0]
    rho_step = hyper_params[1]
    clip_max = hyper_params[2]
    n_total = float(n_rows * n_cols)
    grad_blk = lax.dot_general(x_blk, dy_blk, (((0,), (0,)), ((), ())), preferred_element_type=jnp.float32)
    sq_grad = grad_blk * grad_blk + EPS_ONE
    row_part = jnp.sum(sq_grad, axis=1)
    col_part = jnp.sum(sq_grad, axis=0)
    lead_col = (lax.axis_index(cols_axis) == 0).astype(jnp.float32)
    scalars = jnp.stack([jnp.sum(row_part), jnp.sum(w_blk * w_blk), lead_col * jnp.sum(row_old)])
    row_sum = lax.psum(row_part, cols_axis)
    col_sum = lax.psum(col_part, rows_axis)
    scalar_sum = lax.psum(scalars, BOTH_AXES)
    row_new = beta_two * row_old + (1.0 - beta_two) * (row_sum / n_cols)
    col_new = beta_two * col_old + (1.0 - beta_two) * (col_sum / n_rows)
    row_mean = beta_two * (scalar_sum[2] / n_rows) + (1.0 - beta_two) * (scalar_sum[0] / n_total)
    update = grad_blk * lax.rsqrt((row_new / row_mean)[:, None] * col_new[None, :])
    upd_sq = lax.psum(jnp.sum(update * update), BOTH_AXES)
    upd_rms = jnp.sqrt(upd_sq / n_total)
    w_rms = jnp.sqrt(scalar_sum[1] / n_total)
    step_size = rho_step * jnp.maximum(EPS_TWO, w_rms) / jnp.maximum(1.0, upd_rms / clip_max)
    return w_blk - step_size * update, row_new, col_new


def solution(mesh):
    n_col = mesh.shape['col']
    n_row = mesh.shape['row']
    tile_in = P(None, 'row', 'col')
    tile_out = P(None, 'col', 'row')
    lane_row = P(None, None, 'row')
    lane_col = P(None, None, 'col')
    vec_row = P(None, 'row')
    vec_col = P(None, 'col')

    def local_step(hyper_params, w_in, x_in, dy_in, row_in, col_in, w_out, x_out, dy_out, row_out, col_out):
        d_model = w_in.shape[1] * n_row
        d_hidden = w_in.shape[2] * n_col
        results = []
        for layer_idx in range(w_in.shape[0]):
            in_result = update_block(w_in[layer_idx], x_in[layer_idx], dy_in[layer_idx], row_in[layer_idx], col_in[layer_idx], hyper_params, 'row', 'col', d_model, d_hidden)
            out_result = update_block(w_out[layer_idx], x_out[layer_idx], dy_out[layer_idx], row_out[layer_idx], col_out[layer_idx], hyper_params, 'col', 'row', d_hidden, d_model)
            results.append(in_result + out_result)
        return tuple(jnp.stack([res_item[out_idx] for res_item in results]) for out_idx in range(6))

    return jax.shard_map(local_step, mesh=mesh, in_specs=(P(), tile_in, lane_row, lane_col, vec_row, vec_col, tile_out, lane_col, lane_row, vec_col, vec_row), out_specs=(tile_in, vec_row, vec_col, tile_out, vec_col, vec_row), check_vma=False)
```

profile of v0, /device:TPU:0, one launch (start us, length us, event | category | flops | bytes accessed | tf_op | source)
XLA Modules:
  0.0 241.1 jit_solution(3357510258853510162)
XLA Ops:
  7.2 4.0 %fusion.44 = (f32[256]{0:T(256)S(1)}, f32[2560]{0:T(1024)}, f32[]{:T(128)}, f32[256,2560]{1,0:T(8,128)S(1)}) fusion(bf16[4,512,2560]{2,1,0:T(8,128)(2,1)} %param.14, bf16[4,512,256]{2,1,0:T(8,128)(2,1)} %param.13), kind=kOutput, calls=%fused_computation.86 | convolution fusion | flops 674362624 | bytes 5516292 | tf_op jit(solution)/shard_map/dot_general | solution.py:16
  11.3 5.9 %fusion.41 = (f32[256]{0:T(256)S(1)}, f32[2560]{0:T(1024)}, f32[]{:T(128)}, f32[256,2560]{1,0:T(8,128)}) fusion(bf16[4,512,2560]{2,1,0:T(8,128)(2,1)} %param.14, bf16[4,512,256]{2,1,0:T(8,128)(2,1)} %param.13), kind=kOutput, calls=%fused_computation.83 | convolution fusion | flops 674362624 | bytes 5516292 | tf_op jit(solution)/shard_map/dot_general | solution.py:16
  17.2 3.2 %fusion.50 = (f32[256]{0:T(256)S(1)}, f32[2560]{0:T(1024)}, f32[]{:T(128)}, f32[256,2560]{1,0:T(8,128)}) fusion(bf16[4,512,2560]{2,1,0:T(8,128)(2,1)S(1)} %copy-done.15, bf16[4,512,256]{2,1,0:T(8,128)(2,1)S(1)} %copy-done.17), kind=kOutput, calls=%fused_computation.92 | convolution fusion | flops 674362624 | bytes 5516292 | tf_op jit(solution)/shard_map/dot_general | solution.py:16
  20.4 3.2 %fusion.47 = (f32[256]{0:T(256)S(1)}, f32[2560]{0:T(1024)}, f32[]{:T(128)}, f32[256,2560]{1,0:T(8,128)}) fusion(bf16[4,512,2560]{2,1,0:T(8,128)(2,1)S(1)} %copy-done.15, bf16[4,512,256]{2,1,0:T(8,128)(2,1)S(1)} %copy-done.17), kind=kOutput, calls=%fused_computation.89 | convolution fusion | flops 674362624 | bytes 5516292 | tf_op jit(solution)/shard_map/dot_general | solution.py:16
  23.6 3.2 %fusion.56 = (f32[2560]{0:T(1024)}, f32[256]{0:T(256)S(1)}, f32[]{:T(128)}, f32[2560,256]{1,0:T(8,128)}) fusion(bf16[4,512,256]{2,1,0:T(8,128)(2,1)S(1)} %copy-done.18, bf16[4,512,2560]{2,1,0:T(8,128)(2,1)S(1)} %copy-done.16), kind=kOutput, calls=%fused_computation.98 | convolution fusion | flops 674362624 | bytes 5516292 | tf_op jit(solution)/shard_map/dot_general | solution.py:16
  26.8 3.2 %fusion.53 = (f32[2560]{0:T(1024)}, f32[256]{0:T(256)S(1)}, f32[]{:T(128)}, f32[2560,256]{1,0:T(8,128)}) fusion(bf16[4,512,256]{2,1,0:T(8,128)(2,1)S(1)} %copy-done.18, bf16[4,512,2560]{2,1,0:T(8,128)(2,1)S(1)} %copy-done.16), kind=kOutput, calls=%fused_computation.95 | convolution fusion | flops 674362624 | bytes 5516292 | tf_op jit(solution)/shard_map/dot_general | solution.py:16
  30.0 3.2 %fusion.62 = (f32[2560]{0:T(1024)}, f32[256]{0:T(256)S(1)}, f32[]{:T(128)}, f32[2560,256]{1,0:T(8,128)}) fusion(bf16[4,512,256]{2,1,0:T(8,128)(2,1)S(1)} %copy-done.18, bf16[4,512,2560]{2,1,0:T(8,128)(2,1)S(1)} %copy-done.16), kind=kOutput, calls=%fused_computation.104 | convolution fusion | flops 674362624 | bytes 5516292 | tf_op jit(solution)/shard_map/dot_general | solution.py:16
  33.2 3.2 %fusion.59 = (f32[2560]{0:T(1024)}, f32[256]{0:T(256)S(1)}, f32[]{:T(128)}, f32[2560,256]{1,0:T(8,128)}) fusion(bf16[4,512,256]{2,1,0:T(8,128)(2,1)S(1)} %copy-done.18, bf16[4,512,2560]{2,1,0:T(8,128)(2,1)S(1)} %copy-done.16), kind=kOutput, calls=%fused_computation.101 | convolution fusion | flops 674362624 | bytes 5516292 | tf_op jit(solution)/shard_map/dot_general | solution.py:16
  37.0 5.9 %fusion.30 = (f32[]{:T(128)}, f32[]{:T(128)}, f32[]{:T(128)}, f32[]{:T(128)}) fusion(f32[4,256,2560]{2,1,0:T(8,128)} %param.12), kind=kLoop, calls=%fused_computation.48 | loop fusion | flops 5242876 | bytes 10485776 | tf_op jit(solution)/shard_map/reduce_sum | solution.py:21
  42.9 5.5 %fusion.14 = (f32[]{:T(128)}, f32[]{:T(128)}, f32[]{:T(128)}, f32[]{:T(128)}) fusion(f32[4,2560,256]{2,1,0:T(8,128)} %param.17), kind=kLoop, calls=%fused_computation.24 | loop fusion | flops 5242876 | bytes 10485776 | tf_op jit(solution)/shard_map/reduce_sum | solution.py:21
  48.3 1.3 slice_multiply_fusion.3
  52.1 1.4 multiply_reduce_fusion.11
  55.9 1.3 pad_maximum_fusion.7
  57.2 1.3 pad_maximum_fusion.6
  58.5 1.4 pad_maximum_fusion.9
  59.9 1.3 pad_maximum_fusion.8
  61.2 1.4 pad_maximum_fusion.11
  62.6 1.4 pad_maximum_fusion.10
  64.0 1.2 pad_maximum_fusion.13
  65.2 1.4 pad_maximum_fusion.12
  67.2 34.9 %all-reduce.1 = (f32[3]{0:T(128)S(1)}, f32[3]{0:T(128)S(1)}, f32[3]{0:T(128)S(1)}, f32[3]{0:T(128)S(1)}, f32[3]{0:T(128)S(1)}, /*index=5*/f32[3]{0:T(128)S(1)}, f32[3]{0:T(128)S(1)}, f32[3]{0:T(128)S(1)}) all-reduce(f32[3]{0:T(128)S(1)} %pad_maximum_fusion.9, ...), channel_id=1, replica_groups=mesh['col'=2,'row'=8] {'col','row'}, use_global_device_ids=true, to_apply=%region_33.0 | all-reduce | flops 24 | bytes 192 | tf_op jit(solution)/shard_map/psum | solution.py:24
  112.2 0.7 fusion.83
  112.8 0.7 fusion.82
  114.8 5.2 %all-reduce.3 = (f32[256]{0:T(256)S(1)}, f32[256]{0:T(256)S(1)}, f32[256]{0:T(256)S(1)}, f32[256]{0:T(256)S(1)}, f32[256]{0:T(256)S(1)}, /*index=5*/f32[256]{0:T(256)S(1)}, f32[256]{0:T(256)S(1)}, f32[256]{0:T(256)S(1)}) all-reduce(f32[256]{0:T(256)S(1)} %get-tuple-element.35, ...), channel_id=1, replica_groups=mesh['col'=2,'row'=8] {'col'}, use_global_device_ids=true, to_apply=%region_35.0 | all-reduce | flops 2048 | bytes 16384 | tf_op jit(solution)/shard_map/psum | solution.py:22
  139.2 0.9 broadcast_divide_fusion
  140.1 0.7 broadcast_divide_fusion.1
  140.8 0.7 broadcast_divide_fusion.2
  141.5 0.7 multiply_add_fusion.14
  142.3 0.7 multiply_add_fusion.12
  143.0 0.7 multiply_add_fusion.15
  143.7 0.7 multiply_add_fusion.13
  144.5 3.1 %multiply_reduce_fusion.4 = f32[]{:T(128)} fusion(f32[256,2560]{1,0:T(8,128)} %get-tuple-element.147, f32[2560]{0:T(1024)S(1)} %multiply_add_fusion.12, f32[256]{0:T(256)S(1)} %get-tuple-element.100), kind=kLoop, calls=%fused_computation.66 | loop fusion | flops 2621439 | bytes 2632708 | tf_op jit(solution)/shard_map/reduce_sum | solution.py:29
  147.6 2.0 multiply_reduce_fusion.5
  149.6 2.0 multiply_reduce_fusion.6
  151.6 2.0 multiply_reduce_fusion.7
  153.7 1.4 multiply_reduce_fusion
  155.1 1.5 multiply_reduce_fusion.1
  156.6 1.4 multiply_reduce_fusion.2
  158.0 1.4 multiply_reduce_fusion.3
  159.5 33.3 %all-reduce = (f32[]{:T(128)}, f32[]{:T(128)}, f32[]{:T(128)}, f32[]{:T(128)}, f32[]{:T(128)}, /*index=5*/f32[]{:T(128)}, f32[]{:T(128)}, f32[]{:T(128)}) all-reduce(f32[]{:T(128)} %multiply_reduce_fusion.4, f32[]{:T(128)} %multiply_reduce_fusion.5, f32[]{:T(128)} %multiply_reduce_fusion.6, ...), channel_id=1, replica_groups=mesh['col'=2,'row'=8] {'col','row'}, use_global_device_ids=true, to_apply=%region_39.0 | all-reduce | flops 8 | bytes 64 | tf_op jit(solution)/shard_map/psum | solution.py:29
  202.9 3.7 %fusion.7 = f32[1,2560,256]{2,1,0:T(8,128)} fusion(f32[4,2560,256]{2,1,0:T(8,128)} %param.17, f32[2560,256]{1,0:T(8,128)S(1)} %copy-done.8, f32[]{:T(128)S(6)} %div.309, f32[256]{0:T(256)S(1)} %multiply_add_fusion.17, f32[2560]{0:T(1024)S(1)} %get-tuple-element.90), kind=kLoop, calls=%fused_computation.13 | loop fusion | flops 2621440 | bytes 7875588 | tf_op jit(solution)/shard_map/stack | solution.py:54
  206.7 4.8 %fusion.23 = f32[1,256,2560]{2,1,0:T(8,128)} fusion(f32[4,256,2560]{2,1,0:T(8,128)} %param.12, f32[256,2560]{1,0:T(8,128)} %get-tuple-element.148, f32[]{:T(128)S(6)} %div.269, f32[2560]{0:T(1024)S(1)} %multiply_add_fusion.13, f32[256]{0:T(256)S(1)} %get-tuple-element.98), kind=kLoop, calls=%fused_computation.37 | loop fusion | flops 2621440 | bytes 7875588 | tf_op jit(solution)/shard_map/stack | solution.py:54
  211.7 6.5 %fusion.15 = (f32[1,2560,256]{2,1,0:T(8,128)S(1)}, f32[1,2560,256]{2,1,0:T(8,128)S(1)}, f32[1,2560,256]{2,1,0:T(8,128)S(1)}) fusion(f32[4,2560,256]{2,1,0:T(8,128)} %param.17, f32[2560,256]{1,0:T(8,128)} %get-tuple-element.154, f32[]{:T(128)S(6)} %div.289, f32[256]{0:T(256)S(1)} %multiply_add_fusion.19, f32[2560]{0:T(1024)S(1)} %get-tuple-element.86, ...), kind=kLoop, calls=%fused_computation.25 | loop fusion | flops 7864320 | bytes 23626764 | tf_op jit(solution)/shard_map/stack | solution.py:54
  218.5 1.3 slice-done.2
  219.8 4.5 %fusion.31 = (f32[1,256,2560]{2,1,0:T(8,128)S(1)}, f32[1,256,2560]{2,1,0:T(8,128)S(1)}, f32[1,256,2560]{2,1,0:T(8,128)S(1)}) fusion(f32[4,256,2560]{2,1,0:T(8,128)S(1)} %bitcast.219, f32[256,2560]{1,0:T(8,128)} %get-tuple-element.150, f32[]{:T(128)S(6)} %div.249, f32[2560]{0:T(1024)S(1)} %multiply_add_fusion.15, f32[256]{0:T(256)S(1)} %get-tuple-element.94, ...), kind=kLoop, calls=%fused_computation.49 | loop fusion | flops 7864320 | bytes 23626764 | tf_op jit(solution)/shard_map/stack | solution.py:54
  224.2 0.7 pad_maximum_fusion.3
  225.6 4.4 %pad_maximum_fusion = f32[4,256,2560]{2,1,0:T(8,128)} fusion(f32[1,256,2560]{2,1,0:T(8,128)S(1)} %get-tuple-element.106, f32[1,256,2560]{2,1,0:T(8,128)S(1)} %copy-done.1, f32[1,256,2560]{2,1,0:T(8,128)S(1)} %get-tuple-element.107, f32[1,256,2560]{2,1,0:T(8,128)S(1)} %get-tuple-element.105), kind=kLoop, calls=%fused_computation | loop fusion | flops 7864320 | bytes 20971520 | tf_op jit(solution)/shard_map/stack | solution.py:54
  230.0 4.3 %pad_maximum_fusion.1 = f32[4,2560,256]{2,1,0:T(8,128)} fusion(f32[1,2560,256]{2,1,0:T(8,128)S(1)} %get-tuple-element.103, f32[1,2560,256]{2,1,0:T(8,128)S(1)} %copy-done, f32[1,2560,256]{2,1,0:T(8,128)S(1)} %get-tuple-element.104, f32[1,2560,256]{2,1,0:T(8,128)S(1)} %get-tuple-element.102), kind=kLoop, calls=%fused_computation.1 | loop fusion | flops 7864320 | bytes 20971520 | tf_op jit(solution)/shard_map/stack | solution.py:54
  (74 shorter events, 6.6 us)
Async XLA Ops:
  7.2 132.0 %all-reduce.6.cloned.1.call-start = ((), (), s32[]{:S(2)}) async-start(), calls=%async_computation | async-start | bytes 196608 | tf_op jit(solution)/shard_map/psum | solution.py:23
  7.2 10.0 %copy-start.15 = (bf16[4,512,2560]{2,1,0:T(8,128)(2,1)S(1)}, bf16[4,512,2560]{2,1,0:T(8,128)(2,1)}, u32[]{:S(2)}) copy-start(bf16[4,512,2560]{2,1,0:T(8,128)(2,1)} %param.14) | copy-start | bytes 31457284
  11.2 138.4 %copy-start.2 = (f32[256,2560]{1,0:T(8,128)}, f32[256,2560]{1,0:T(8,128)S(1)}, u32[]{:S(2)}) copy-start(f32[256,2560]{1,0:T(8,128)S(1)} %get-tuple-element.149) | copy-start | bytes 7864324
  11.2 5.9 %copy-start.17 = (bf16[4,512,256]{2,1,0:T(8,128)(2,1)S(1)}, bf16[4,512,256]{2,1,0:T(8,128)(2,1)}, u32[]{:S(2)}) copy-start(bf16[4,512,256]{2,1,0:T(8,128)(2,1)} %param.13) | copy-start | bytes 3145732
  17.2 6.4 %copy-start.16 = (bf16[4,512,2560]{2,1,0:T(8,128)(2,1)S(1)}, bf16[4,512,2560]{2,1,0:T(8,128)(2,1)}, u32[]{:S(2)}) copy-start(bf16[4,512,2560]{2,1,0:T(8,128)(2,1)} %param.18) | copy-start | bytes 31457284
  20.4 3.2 %copy-start.18 = (bf16[4,512,256]{2,1,0:T(8,128)(2,1)S(1)}, bf16[4,512,256]{2,1,0:T(8,128)(2,1)}, u32[]{:S(2)}) copy-start(bf16[4,512,256]{2,1,0:T(8,128)(2,1)} %param.19) | copy-start | bytes 3145732
  33.2 3.2 %copy-start.12 = (f32[3]{0:T(128)S(1)}, f32[3]{0:T(128)}, u32[]{:S(2)}) copy-start(f32[3]{0:T(128)} %param.11) | copy-start | bytes 40
  42.8 5.5 %copy-start.13 = (f32[4,256]{1,0:T(4,128)S(1)}, f32[4,256]{1,0:T(4,128)}, u32[]{:S(2)}) copy-start(f32[4,256]{1,0:T(4,128)} %param.21) | copy-start | bytes 12292
  42.8 5.5 %copy-start.14 = (f32[4,256]{1,0:T(4,128)S(1)}, f32[4,256]{1,0:T(4,128)}, u32[]{:S(2)}) copy-start(f32[4,256]{1,0:T(4,128)} %param.15) | copy-start | bytes 12292
  42.9 9.2 %copy-start.9 = (f32[4,2560]{1,0:T(4,128)S(1)}, f32[4,2560]{1,0:T(4,128)}, u32[]{:S(2)}) copy-start(f32[4,2560]{1,0:T(4,128)} %param.20) | copy-start | bytes 122884
  42.9 9.2 %copy-start.10 = (f32[4,2560]{1,0:T(4,128)S(1)}, f32[4,2560]{1,0:T(4,128)}, u32[]{:S(2)}) copy-start(f32[4,2560]{1,0:T(4,128)} %param.16) | copy-start | bytes 122884
  139.2 8.4 %copy-start.7 = (f32[256,2560]{1,0:T(8,128)S(1)}, f32[256,2560]{1,0:T(8,128)}, u32[]{:S(2)}) copy-start(f32[256,2560]{1,0:T(8,128)} %get-tuple-element.148) | copy-start | bytes 7864324
  147.6 4.1 %copy-start.3 = (f32[256,2560]{1,0:T(8,128)S(1)}, f32[256,2560]{1,0:T(8,128)}, u32[]{:S(2)}) copy-start(f32[256,2560]{1,0:T(8,128)} %get-tuple-element.150) | copy-start | bytes 7864324
  149.6 4.1 %copy-start.6 = (f32[2560,256]{1,0:T(8,128)S(1)}, f32[2560,256]{1,0:T(8,128)}, u32[]{:S(2)}) copy-start(f32[2560,256]{1,0:T(8,128)} %get-tuple-element.151) | copy-start | bytes 7864324
  151.6 3.5 %copy-start.8 = (f32[2560,256]{1,0:T(8,128)S(1)}, f32[2560,256]{1,0:T(8,128)}, u32[]{:S(2)}) copy-start(f32[2560,256]{1,0:T(8,128)} %get-tuple-element.152) | copy-start | bytes 7864324
  153.7 2.9 %copy-start.4 = (f32[2560,256]{1,0:T(8,128)S(1)}, f32[2560,256]{1,0:T(8,128)}, u32[]{:S(2)}) copy-start(f32[2560,256]{1,0:T(8,128)} %get-tuple-element.153) | copy-start | bytes 7864324
  155.1 2.9 %copy-start.11 = (f32[2560]{0:T(1024)S(1)}, f32[2560]{0:T(1024)}, u32[]{:S(2)}) copy-start(f32[2560]{0:T(1024)} %get-tuple-element.77) | copy-start | bytes 30724
  155.1 2.9 %copy-start.5 = (f32[2560,256]{1,0:T(8,128)S(1)}, f32[2560,256]{1,0:T(8,128)}, u32[]{:S(2)}) copy-start(f32[2560,256]{1,0:T(8,128)} %get-tuple-element.154) | copy-start | bytes 7864324
  206.7 11.6 %slice-start = ((s8[10485760]{0:T(1024)(128)(4,1)}), s8[2097152]{0:T(1024)(128)(4,1)S(1)}, s32[]{:S(2)}) async-start(s8[10485760]{0:T(1024)(128)(4,1)} %bitcast.218), calls=%async_computation.1 | async-start | bytes 4194304
  211.7 6.7 %slice-start.1 = ((s8[10485760]{0:T(1024)(128)(4,1)}), s8[4194304]{0:T(1024)(128)(4,1)S(1)}, s32[]{:S(2)}) async-start(s8[10485760]{0:T(1024)(128)(4,1)} %bitcast.218), calls=%async_computation.2 | async-start | bytes 8388608
  211.7 8.0 %slice-start.2 = ((s8[10485760]{0:T(1024)(128)(4,1)}), s8[4194304]{0:T(1024)(128)(4,1)S(1)}, s32[]{:S(2)}) async-start(s8[10485760]{0:T(1024)(128)(4,1)} %bitcast.218), calls=%async_computation.3 | async-start | bytes 8388608
  219.8 5.8 %copy-start.1 = (f32[1,256,2560]{2,1,0:T(8,128)S(1)}, f32[1,256,2560]{2,1,0:T(8,128)}, u32[]{:S(2)}) copy-start(f32[1,256,2560]{2,1,0:T(8,128)} %fusion.23) | copy-start | bytes 7864324
  225.6 4.4 %copy-start = (f32[1,2560,256]{2,1,0:T(8,128)S(1)}, f32[1,2560,256]{2,1,0:T(8,128)}, u32[]{:S(2)}) copy-start(f32[1,2560,256]{2,1,0:T(8,128)} %fusion.7) | copy-start | bytes 7864324
Sparse Core Ops, SparseCore 0:
  36.5 50.4 all-reduce.5
where the time goes:
time: 243 us; the launch traced here: 241 us
  other arithmetic  75.5 us (31%)
  blocking collectives  73.4 us (30%)
  between operations  55.8 us (23%)
  matrix products  29.1 us (12%)
  local copies, waits for them, and re-layouts  7.21 us (3%)
    psum x1, blocking collectives, update_block(): scalar_sum = lax.psum(scalars, BOTH_AXES)  34.9 us
    psum x1, blocking collectives, update_block(): upd_sq = lax.psum(jnp.sum(update * update), BOTH_AXES)  33.3 us
    another operation x10, other arithmetic, local_step(): jnp.stack([res_item[out_idx] for res_item in results])  30.8 us
    dot_general x8, matrix products, update_block(): lax.dot_general(x_blk, dy_blk, (((0,), (0,)), ((), ())), preferred_elemen...  29.1 us
    reduce_sum x8, other arithmetic, update_block(): upd_sq = lax.psum(jnp.sum(update * update), BOTH_AXES)  14.9 us
    reduce_sum x2, other arithmetic, update_block(): jnp.sum(w_blk * w_blk)  11.3 us
    another operation x8, other arithmetic, update_block(): jnp.stack([jnp.sum(row_part), jnp.sum(w_blk * w_blk), lead_col * jnp.sum(...  10.6 us
    psum x1, blocking collectives, update_block(): row_sum = lax.psum(row_part, cols_axis)  5.21 us
  transfers between devices with their start and end apart: 1, of which 0 were waited for; matrix products, arithmetic and copies ran while one was open for 13% of the time, Pallas kernels for 0%

commit v1 on v0

v1 whole, which is shorter than its diff:
```python
import functools

import jax
import jax.numpy as jnp
from jax import lax
from jax.experimental import pallas as pl
from jax.experimental.pallas import tpu as pltpu
from jax.sharding import PartitionSpec as P

EPS_ONE = 1e-30
EPS_TWO = 1e-3
LANE = 128
CHUNK = 256
MESH = pl.DeviceIdType.MESH
F32 = jnp.float32


def stats_kernel(dims, hyper_hbm, w_in, x_in, dy_in, row_in, col_in, w_out, x_out, dy_out, row_out, col_out,
                 grad, wv_in, wv_out, short_new, long_new, scal,
                 act_s, act_l, lhs_t, old_s_in, old_l_in, old_s_out, old_l_out, short_old, long_old,
                 long_buf, short_buf, fin_buf, racc, cacc, rscale, linv, pack, hyper_ref,
                 act_sem, w_sem, old_sem, long_send, long_recv, short_send, short_recv, fin_send, fin_recv):
    n_col, n_row, layers, ms, ml, d_model, d_hidden = dims
    n_dev = n_col * n_row
    sch, lch = ms // LANE, ml // LANE
    my_col = lax.axis_index('col')
    my_row = lax.axis_index('row')

    def act_copies(layer, kind):
        slot = 2 * lax.rem(layer, 2) + kind
        src_s = (x_in, dy_out)[kind]
        src_l = (dy_in, x_out)[kind]
        return (pltpu.make_async_copy(src_s.at[layer], act_s.at[slot], act_sem.at[slot, 0]),
                pltpu.make_async_copy(src_l.at[layer], act_l.at[slot], act_sem.at[slot, 1]))

    def w_copy(layer, kind):
        src = (w_in, w_out)[kind]
        dst = (wv_in, wv_out)[kind]
        return pltpu.make_async_copy(src.at[layer], dst.at[layer], w_sem.at[layer, kind])

    old_copies = [pltpu.make_async_copy(src, dst, old_sem.at[idx]) for idx, (src, dst) in enumerate(
        ((row_in, old_s_in), (col_in, old_l_in), (col_out, old_s_out), (row_out, old_l_out), (hyper_hbm, hyper_ref)))]

    for layer in range(2):
        for kind in range(2):
            for copy in act_copies(layer, kind):
                copy.start()
    for copy in old_copies:
        copy.start()

    barrier = pltpu.get_barrier_semaphore()

    def peer_of(step):
        lin = lax.rem(my_col * n_row + my_row + step, n_dev)
        return (lin // n_row, lax.rem(lin, n_row))

    for step in range(1, n_dev):
        pl.semaphore_signal(barrier, inc=1, device_id=peer_of(step), device_id_type=MESH)

    pack[...] = jnp.zeros_like(pack)
    for copy in old_copies:
        copy.wait()
    beta_two = hyper_ref[0]
    for kind, (src_s, src_l) in enumerate(((old_s_in, old_l_in), (old_s_out, old_l_out))):
        for layer in range(layers):
            for j in range(sch):
                short_old[2 * layer + kind, j:j + 1, :] = src_s[layer:layer + 1, j * LANE:(j + 1) * LANE]
            for j in range(lch):
                long_old[2 * layer + kind, j:j + 1, :] = src_l[layer:layer + 1, j * LANE:(j + 1) * LANE]
    pl.semaphore_wait(barrier, n_dev - 1)

    def long_copy(mat, step):
        peer = lax.rem(my_row + step, n_row)
        return pltpu.make_async_remote_copy(
            src_ref=long_buf.at[mat, my_row], dst_ref=long_buf.at[mat, my_row],
            send_sem=long_send.at[mat], recv_sem=long_recv.at[mat],
            device_id=(my_col, peer), device_id_type=MESH)

    def short_copy(mat):
        return pltpu.make_async_remote_copy(
            src_ref=short_buf.at[mat, my_col], dst_ref=short_buf.at[mat, my_col],
            send_sem=short_send.at[mat], recv_sem=short_recv.at[mat],
            device_id=(n_col - 1 - my_col, my_row), device_id_type=MESH)

    def form_grad(layer, kind):
        mat = 2 * layer + kind
        slot = 2 * lax.rem(layer, 2) + kind
        for copy in act_copies(layer, kind):
            copy.wait()
        lhs_t[...] = act_s[slot].T
        racc[...] = jnp.zeros_like(racc)

        def chunk(c, carry):
            cols = pl.ds(pl.multiple_of(c * CHUNK, CHUNK), CHUNK)
            g = jnp.dot(lhs_t[...], act_l[slot, :, cols], preferred_element_type=F32)
            grad[mat, :, cols] = g
            sq = g * g
            racc[...] += sq[:, :LANE] + sq[:, LANE:]
            cacc[:, cols] = jnp.sum(sq.reshape(ms // 8, 8, CHUNK), axis=0)
            return carry

        lax.fori_loop(0, ml // CHUNK, chunk, 0)
        for j in range(lch):
            long_buf[mat, my_row, j:j + 1, :] = jnp.sum(cacc[:, j * LANE:(j + 1) * LANE], axis=0, keepdims=True)
        for j in range(sch):
            part = racc[j * LANE:(j + 1) * LANE, :].T
            short_buf[mat, my_col, j:j + 1, :] = jnp.sum(part, axis=0, keepdims=True)
        for step in range(1, n_row):
            long_copy(mat, step).start()
        short_copy(mat).start()

    def put(lane, value):
        at = lax.broadcasted_iota(jnp.int32, (1, LANE), 1) == lane
        pack[...] += jnp.where(at, value, 0.0)

    def total(value):
        return jnp.sum(jnp.sum(value, axis=1, keepdims=True), axis=0, keepdims=True)

    def update_sq(layer, kind):
        mat = 2 * layer + kind
        pltpu.make_async_copy(long_buf.at[mat, pl.ds(0, n_row - 1)], long_buf.at[mat, pl.ds(0, n_row - 1)],
                              long_recv.at[mat]).wait()
        short_copy(mat).wait_recv()
        lsum = long_buf[mat, 0]
        for dev in range(1, n_row):
            lsum = lsum + long_buf[mat, dev]
        ssum = short_buf[mat, 0]
        for dev in range(1, n_col):
            ssum = ssum + short_buf[mat, dev]
        lnew = beta_two * long_old[mat] + (1.0 - beta_two) * (lsum * (1.0 / d_model) + EPS_ONE)
        snew = beta_two * short_old[mat] + (1.0 - beta_two) * (ssum * (1.0 / d_hidden) + EPS_ONE)
        long_new[mat] = lnew
        short_new[mat] = snew
        if kind == 0:
            rho = total(snew)
            rs = lax.rsqrt(snew / (rho * (1.0 / ms)))
            linv[...] = 1.0 / lnew
        else:
            rho = total(lnew)
            rs = lax.rsqrt(snew)
            linv[...] = (rho * (1.0 / ml)) / lnew
        for j in range(sch):
            rscale[j * LANE:(j + 1) * LANE, :] = jnp.broadcast_to(rs[j:j + 1, :], (LANE, LANE)).T

        def chunk(c, acc):
            scale = rscale[...]
            for h in range(CHUNK // LANE):
                j = c * (CHUNK // LANE) + h
                u = grad[mat, :, pl.ds(pl.multiple_of(j * LANE, LANE), LANE)] * scale
                part = jnp.sum((u * u).reshape(ms // 8, 8, LANE), axis=0)
                acc = acc + part * linv[pl.ds(j, 1), :]
            return acc

        acc = lax.fori_loop(0, ml // CHUNK, chunk, jnp.zeros((8, LANE), F32))
        put(mat, total(acc))
        put(mat + 2 * layers, rho)

    def weight_sq(layer, kind):
        mat = 2 * layer + kind
        w_copy(layer, kind).wait()
        ref = (wv_in, wv_out)[kind]
        rows, cols = ref.shape[1:]
        block = max(8, 8 * 8 * 20 * LANE // cols)

        def chunk(t, acc):
            v = ref[layer, pl.ds(pl.multiple_of(t * block, 8), block), :]
            v = v * v
            part = v[:, :LANE]
            for j in range(1, cols // LANE):
                part = part + v[:, j * LANE:(j + 1) * LANE]
            return acc + jnp.sum(part.reshape(block // 8, 8, LANE), axis=0)

        acc = lax.fori_loop(0, rows // block, chunk, jnp.zeros((8, LANE), F32))
        put(mat + 4 * layers, total(acc))

    def phase_one(layer, carry):
        for kind in range(2):
            form_grad(layer, kind)

            @pl.when(layer + 2 < layers)
            def _():
                for copy in act_copies(layer + 2, kind):
                    copy.start()

            w_copy(layer, kind).start()

        @pl.when(layer >= 2)
        def _():
            for kind in range(2):
                update_sq(layer - 2, kind)

        return carry

    lax.fori_loop(0, layers, phase_one, 0)

    def phase_two(layer, carry):
        @pl.when(layer >= layers - 2)
        def _():
            for kind in range(2):
                update_sq(layer, kind)

        for kind in range(2):
            weight_sq(layer, kind)
        return carry

    lax.fori_loop(0, layers, phase_two, 0)

    me = my_col * n_row + my_row
    fin_buf[me] = pack[...]

    def fin_copy(step):
        return pltpu.make_async_remote_copy(
            src_ref=fin_buf.at[me], dst_ref=fin_buf.at[me], send_sem=fin_send, recv_sem=fin_recv,
            device_id=peer_of(step), device_id_type=MESH)

    for step in range(1, n_dev):
        fin_copy(step).start()
    for mat in range(2 * layers):
        pltpu.make_async_copy(long_buf.at[mat, pl.ds(0, n_row - 1)], long_buf.at[mat, pl.ds(0, n_row - 1)],
                              long_send.at[mat]).wait()
        short_copy(mat).wait_send()
    others = fin_buf.at[pl.ds(0, n_dev - 1)]
    pltpu.make_async_copy(others, others, fin_send).wait()
    pltpu.make_async_copy(others, others, fin_recv).wait()

    lane = lax.broadcasted_iota(jnp.int32, (1, LANE), 1)
    is_in = lax.rem(lane, 2) == 0
    valid = lane < 2 * layers
    rho_sum = jnp.zeros((1, LANE), F32)
    w_sq = jnp.zeros((1, LANE), F32)
    for dev in range(n_dev):
        rho_sum = rho_sum + pltpu.roll(fin_buf[dev], LANE - 2 * layers, 1)
        w_sq = w_sq + pltpu.roll(fin_buf[dev], LANE - 4 * layers, 1)
    row_mean = rho_sum * jnp.where(is_in, 1.0 / (n_col * d_model), 1.0 / (n_row * d_hidden))
    row_mean = jnp.where(valid, row_mean, 1.0)
    upd_sq = jnp.zeros((1, LANE), F32)
    for dev in range(n_dev):
        sigma = pltpu.roll(fin_buf[dev], LANE - 2 * layers, 1) * jnp.where(is_in, 1.0 / ms, 1.0 / ml)
        upd_sq = upd_sq + fin_buf[dev] * (row_mean / jnp.where(valid, sigma, 1.0))
    n_total = float(d_model * d_hidden)
    upd_rms = jnp.sqrt(jnp.where(valid, upd_sq, 0.0) * (1.0 / n_total))
    w_rms = jnp.sqrt(jnp.where(valid, w_sq, 0.0) * (1.0 / n_total))
    size = hyper_ref[1] * jnp.maximum(EPS_TWO, w_rms) / jnp.maximum(1.0, upd_rms / hyper_ref[2])
    scal[0:1, :] = row_mean
    scal[1:2, :] = size


def write_kernel(dims, grad, wv_in, wv_out, short_new, long_new, scal,
                 w_in_new, row_in_new, col_in_new, w_out_new, row_out_new, col_out_new,
                 stage_in, stage_out, pscale, qscale, sem_in, sem_out):
    layers, ms, ml, parts = dims
    sch, lch = ms // LANE, ml // LANE
    rows_in, rows_out = ms // parts, ml // parts

    for layer in range(layers):
        for kind, (out_s, out_l) in enumerate(((row_in_new, col_in_new), (col_out_new, row_out_new))):
            mat = 2 * layer + kind
            for j in range(sch):
                out_s[layer:layer + 1, j * LANE:(j + 1) * LANE] = short_new[mat, j:j + 1, :]
            for j in range(lch):
                out_l[layer:layer + 1, j * LANE:(j + 1) * LANE] = long_new[mat, j:j + 1, :]

    def out_copy(layer, kind, part):
        if kind == 0:
            return pltpu.make_async_copy(
                stage_in.at[part], w_in_new.at[layer, pl.ds(part * rows_in, rows_in)], sem_in.at[part])
        return pltpu.make_async_copy(
            stage_out.at[part], w_out_new.at[layer, pl.ds(part * rows_out, rows_out)], sem_out.at[part])

    def pick(row, mat):
        at = lax.broadcasted_iota(jnp.int32, (1, LANE), 1) == mat
        return jnp.sum(jnp.where(at, scal[row:row + 1, :], 0.0), axis=1, keepdims=True)

    def scales(mat, kind):
        row_mean = pick(0, mat)
        size = pick(1, mat)
        if kind == 0:
            p = size * lax.rsqrt(short_new[mat] / row_mean)
            qscale[...] = lax.rsqrt(long_new[mat])
        else:
            p = size * lax.rsqrt(short_new[mat])
            qscale[...] = lax.rsqrt(long_new[mat] / row_mean)
        for j in range(sch):
            pscale[j * LANE:(j + 1) * LANE, :] = jnp.broadcast_to(p[j:j + 1, :], (LANE, LANE)).T

    def one_layer(layer, carry):
        scales(2 * layer, 0)
        for part in range(parts):
            @pl.when(layer > 0)
            def _():
                out_copy(layer, 0, part).wait()

            r0 = part * rows_in

            def cols_in(j, inner):
                cols = pl.ds(pl.multiple_of(j * LANE, LANE), LANE)
                u = grad[2 * layer, r0:r0 + rows_in, cols] * pscale[r0:r0 + rows_in, :] * qscale[pl.ds(j, 1), :]
                stage_in[part, :, cols] = wv_in[layer, r0:r0 + rows_in, cols] - u
                return inner

            lax.fori_loop(0, lch, cols_in, 0)
            out_copy(layer, 0, part).start()

        scales(2 * layer + 1, 1)
        for part in range(parts):
            @pl.when(layer > 0)
            def _():
                out_copy(layer, 1, part).wait()

            j0 = part * (rows_out // LANE)

            def rows_loop(j, inner):
                cols = pl.ds(pl.multiple_of((j0 + j) * LANE, LANE), LANE)
                rows = pl.ds(pl.multiple_of(j * LANE, LANE), LANE)
                u = grad[2 * layer + 1, :, cols] * pscale[...] * qscale[pl.ds(j0 + j, 1), :]
                stage_out[part, rows, :] = wv_out[layer, cols, :] - u.T
                return inner

            lax.fori_loop(0, rows_out // LANE, rows_loop, 0)
            out_copy(layer, 1, part).start()
        return carry

    lax.fori_loop(0, layers, one_layer, 0)
    for kind in range(2):
        for part in range(parts):
            out_copy(layers - 1, kind, part).wait()


def solution(mesh):
    n_col = mesh.shape['col']
    n_row = mesh.shape['row']
    tile_in = P(None, 'row', 'col')
    tile_out = P(None, 'col', 'row')
    lane_row = P(None, None, 'row')
    lane_col = P(None, None, 'col')
    vec_row = P(None, 'row')
    vec_col = P(None, 'col')

    def local_step(hyper_params, w_in, x_in, dy_in, row_in, col_in, w_out, x_out, dy_out, row_out, col_out):
        layers, ms, ml = w_in.shape
        tokens = x_in.shape[1]
        mats = 2 * layers
        sch, lch = ms // LANE, ml // LANE
        n_dev = n_col * n_row
        d_model, d_hidden = ms * n_row, ml * n_col
        hbm_spec = pl.BlockSpec(memory_space=pltpu.HBM)
        vmem_spec = pl.BlockSpec(memory_space=pltpu.VMEM)
        dims = (n_col, n_row, layers, ms, ml, d_model, d_hidden)
        bf16 = jnp.bfloat16
        kept = pl.pallas_call(
            functools.partial(stats_kernel, dims),
            out_shape=(pltpu.VMEM((mats, ms, ml), F32), pltpu.VMEM((layers, ms, ml), F32),
                       pltpu.VMEM((layers, ml, ms), F32), pltpu.VMEM((mats, sch, LANE), F32),
                       pltpu.VMEM((mats, lch, LANE), F32), pltpu.VMEM((8, LANE), F32)),
            in_specs=[hbm_spec] * 11,
            out_specs=(vmem_spec,) * 6,
            scratch_shapes=[
                pltpu.VMEM((4, tokens, ms), bf16), pltpu.VMEM((4, tokens, ml), bf16),
                pltpu.VMEM((ms, tokens), bf16),
                pltpu.VMEM((layers, ms), F32), pltpu.VMEM((layers, ml), F32),
                pltpu.VMEM((layers, ms), F32), pltpu.VMEM((layers, ml), F32),
                pltpu.VMEM((mats, sch, LANE), F32), pltpu.VMEM((mats, lch, LANE), F32),
                pltpu.VMEM((mats, n_row, lch, LANE), F32), pltpu.VMEM((mats, n_col, sch, LANE), F32),
                pltpu.VMEM((n_dev, 1, LANE), F32),
                pltpu.VMEM((ms, LANE), F32), pltpu.VMEM((8, ml), F32), pltpu.VMEM((ms, LANE), F32),
                pltpu.VMEM((lch, LANE), F32), pltpu.VMEM((1, LANE), F32), pltpu.SMEM((3,), F32),
                pltpu.SemaphoreType.DMA((4, 2)), pltpu.SemaphoreType.DMA((layers, 2)),
                pltpu.SemaphoreType.DMA((5,)),
                pltpu.SemaphoreType.DMA((mats,)), pltpu.SemaphoreType.DMA((mats,)),
                pltpu.SemaphoreType.DMA((mats,)), pltpu.SemaphoreType.DMA((mats,)),
                pltpu.SemaphoreType.DMA, pltpu.SemaphoreType.DMA,
            ],
            compiler_params=pltpu.CompilerParams(
                collective_id=0, has_side_effects=True, vmem_limit_bytes=13 * 2 ** 20),
            name='stats',
        )(*(pltpu.with_memory_space_constraint(item, pltpu.HBM) for item in (
            hyper_params, w_in, x_in, dy_in, row_in, col_in, w_out, x_out, dy_out, row_out, col_out)))
        parts = 4
        return pl.pallas_call(
            functools.partial(write_kernel, (layers, ms, ml, parts)),
            out_shape=tuple(jax.ShapeDtypeStruct(item.shape, F32) for item in (
                w_in, row_in, col_in, w_out, row_out, col_out)),
            in_specs=[vmem_spec] * 6,
            out_specs=(hbm_spec, vmem_spec, vmem_spec, hbm_spec, vmem_spec, vmem_spec),
            scratch_shapes=[
                pltpu.VMEM((parts, ms // parts, ml), F32), pltpu.VMEM((parts, ml // parts, ms), F32),
                pltpu.VMEM((ms, LANE), F32), pltpu.VMEM((lch, LANE), F32),
                pltpu.SemaphoreType.DMA((parts,)), pltpu.SemaphoreType.DMA((parts,)),
            ],
            compiler_params=pltpu.CompilerParams(vmem_limit_bytes=13 * 2 ** 20),
            name='write',
        )(*kept)

    return jax.shard_map(local_step, mesh=mesh, in_specs=(P(), tile_in, lane_row, lane_col, vec_row, vec_col, tile_out, lane_col, lane_row, vec_col, vec_row), out_specs=(tile_in, vec_row, vec_col, tile_out, vec_col, vec_row), check_vma=False)
```

time: 243 us -> 58.2 us (0.24)
  other arithmetic: 75.5 us -> 0 us
  blocking collectives: 73.4 us -> 0 us
  Pallas kernels: 0 us -> 57.4 us
  between operations: 55.8 us -> 0.64 us
  matrix products: 29.1 us -> 0 us
  local copies, waits for them, and re-layouts: 7.21 us -> 0 us
    psum x3 -> x0, blocking collectives: 73.4 us -> none  [the longest x1 34.9 us: update_block(): scalar_sum = lax.psum(scalars, BOTH_AXES)]
    pallas_call x0 -> x2, Pallas kernels: none -> 57.4 us  [the longest x1 41.1 us: local_step(): pl.pallas_call(functools.partial(stats_kernel, dims), out_shape=(pltpu.VM...]
    another operation x18 -> x0, other arithmetic: 41.4 us -> none  [the longest x10 30.8 us: local_step(): jnp.stack([res_item[out_idx] for res_item in results])]
    dot_general x8 -> x0, matrix products: 29.1 us -> none  [update_block(): lax.dot_general(x_blk, dy_blk, (((0,), (0,)), ((), ())), preferred_elemen...]
    reduce_sum x10 -> x0, other arithmetic: 26.2 us -> none  [the longest x8 14.9 us: update_block(): upd_sq = lax.psum(jnp.sum(update * update), BOTH_AXES)]
    slice x9 -> x0, local copies, waits for them, and re-layouts: 5.6 us -> none  [the longest x7 4.42 us: update_block(): w_rms = jnp.sqrt(scalar_sum[1] / n_total)]
    add x8 -> x0, other arithmetic: 2.88 us -> none  [update_block(): col_new = beta_two * col_old + (1.0 - beta_two) * (col_sum / n_rows)]
    mul x2 -> x0, other arithmetic: 2.62 us -> none  [the longest x1 1.37 us: update_block(): row_new = beta_two * row_old + (1.0 - beta_two) * (row_sum / n_cols)]
  transfers between devices with their start and end apart: 1 -> 0, of which waited for: 0 -> 0; matrix products, arithmetic and copies ran while one was open for 13% -> 0% of each run, Pallas kernels for 0% -> 0%
where the time goes in v1:
time: 58.2 us; the launch traced here: 58.1 us
  Pallas kernels  57.4 us (99%)
  between operations  0.64 us (1%)
    pallas_call x1, Pallas kernels, local_step(): pl.pallas_call(functools.partial(stats_kernel, dims), out_shape=(pltpu.VM...  41.1 us
    pallas_call x1, Pallas kernels, local_step(): pl.pallas_call(functools.partial(write_kernel, (layers, ms, ml, parts)),...  16.3 us

profile of v1, /device:TPU:0, one launch (start us, length us, event | category | flops | bytes accessed | tf_op | source)
XLA Modules:
  0.0 58.1 jit_solution(5407496094969535861)
XLA Ops:
  0.6 41.1 %stats.1 = (f32[8,256,2560]{2,1,0:T(8,128)S(1)}, f32[4,256,2560]{2,1,0:T(8,128)S(1)}, f32[4,2560,256]{2,1,0:T(8,128)S(1)}, f32[8,2,128]{2,1,0:T(2,128)S(1)}, f32...) custom-call(f32[3]{0:T(128)} %hyper_hbm.1, f32[4,256,2560]{2,1,0:T(8,128)} %w_in.1, bf16[4,512,256]{2,1,0:T(8,128)(2,1)} %x_in.1, ...), custom_call_target="tpu_custom_call" | custom-call | tf_op jit(solution)/shard_map/stats/pallas_call | solution.py:350
  41.8 16.3 %write.1 = (f32[4,256,2560]{2,1,0:T(8,128)}, f32[4,256]{1,0:T(4,128)}, f32[4,2560]{1,0:T(4,128)}, f32[4,2560,256]{2,1,0:T(8,128)}, f32[4,2560]{1,0:T(4,128)}, /*index=5*/f32[4,256]{1,0:T(4,128)}) custom-call(f32[8,256,2560]{2,1,0:T(8,128)S(1)} %get-tuple-element.12.grad, f32[4,256,2560]{2,1,0:T(8,128)S(1)} %get-tuple-element.13.wv_in, ...), custom_call_target="tpu_custom_call" | custom-call | tf_op jit(solution)/shard_map/write/pallas_call | solution.py:379

commit v2 on v1

--- a/solution.py
+++ b/solution.py
@@ -10,9 +10,17 @@
 EPS_ONE = 1e-30
 EPS_TWO = 1e-3
 LANE = 128
-CHUNK = 256
+CHUNK = 1280
+UCOLS = 640
+WCOLS = 512
 MESH = pl.DeviceIdType.MESH
 F32 = jnp.float32
+
+
+def tree(items):
+    while len(items) > 1:
+        items = [items[k] + items[k + 1] if k + 1 < len(items) else items[k] for k in range(0, len(items), 2)]
+    return items[0]
 
 
 def stats_kernel(dims, hyper_hbm, w_in, x_in, dy_in, row_in, col_in, w_out, x_out, dy_out, row_out, col_out,
@@ -95,7 +103,7 @@
             g = jnp.dot(lhs_t[...], act_l[slot, :, cols], preferred_element_type=F32)
             grad[mat, :, cols] = g
             sq = g * g
-            racc[...] += sq[:, :LANE] + sq[:, LANE:]
+            racc[...] += tree([sq[:, j * LANE:(j + 1) * LANE] for j in range(CHUNK // LANE)])
             cacc[:, cols] = jnp.sum(sq.reshape(ms // 8, 8, CHUNK), axis=0)
             return carry
 
@@ -144,14 +152,14 @@
 
         def chunk(c, acc):
             scale = rscale[...]
-            for h in range(CHUNK // LANE):
-                j = c * (CHUNK // LANE) + h
+            for h in range(UCOLS // LANE):
+                j = c * (UCOLS // LANE) + h
                 u = grad[mat, :, pl.ds(pl.multiple_of(j * LANE, LANE), LANE)] * scale
                 part = jnp.sum((u * u).reshape(ms // 8, 8, LANE), axis=0)
                 acc = acc + part * linv[pl.ds(j, 1), :]
             return acc
 
-        acc = lax.fori_loop(0, ml // CHUNK, chunk, jnp.zeros((8, LANE), F32))
+        acc = lax.fori_loop(0, ml // UCOLS, chunk, jnp.zeros((8, LANE), F32))
         put(mat, total(acc))
         put(mat + 2 * layers, rho)
 
@@ -165,10 +173,9 @@
         def chunk(t, acc):
             v = ref[layer, pl.ds(pl.multiple_of(t * block, 8), block), :]
             v = v * v
-            part = v[:, :LANE]
-            for j in range(1, cols // LANE):
-                part = part + v[:, j * LANE:(j + 1) * LANE]
-            return acc + jnp.sum(part.reshape(block // 8, 8, LANE), axis=0)
+            part = tree([v[:, j * LANE:(j + 1) * LANE] for j in range(cols // LANE)])
+            part = [part[8 * j:8 * j + 8] for j in range(block // 8)]
+            return acc + tree(part)
 
         acc = lax.fori_loop(0, rows // block, chunk, jnp.zeros((8, LANE), F32))
         put(mat + 4 * layers, total(acc))
@@ -247,25 +254,20 @@
 
 def write_kernel(dims, grad, wv_in, wv_out, short_new, long_new, scal,
                  w_in_new, row_in_new, col_in_new, w_out_new, row_out_new, col_out_new,
-                 stage_in, stage_out, pscale, qscale, sem_in, sem_out):
+                 stage_in, stage_out, pscale, qscale, vec_s, vec_l, sem_in, sem_out, sem_vec):
     layers, ms, ml, parts = dims
     sch, lch = ms // LANE, ml // LANE
     rows_in, rows_out = ms // parts, ml // parts
 
-    for layer in range(layers):
-        for kind, (out_s, out_l) in enumerate(((row_in_new, col_in_new), (col_out_new, row_out_new))):
-            mat = 2 * layer + kind
-            for j in range(sch):
-                out_s[layer:layer + 1, j * LANE:(j + 1) * LANE] = short_new[mat, j:j + 1, :]
-            for j in range(lch):
-                out_l[layer:layer + 1, j * LANE:(j + 1) * LANE] = long_new[mat, j:j + 1, :]
+    vec_copies = [pltpu.make_async_copy(src, dst, sem_vec.at[idx]) for idx, (src, dst) in enumerate(
+        ((vec_s.at[0], row_in_new), (vec_l.at[0], col_in_new), (vec_s.at[1], col_out_new), (vec_l.at[1], row_out_new)))]
 
     def out_copy(layer, kind, part):
         if kind == 0:
-            return pltpu.make_async_copy(
-                stage_in.at[part], w_in_new.at[layer, pl.ds(part * rows_in, rows_in)], sem_in.at[part])
-        return pltpu.make_async_copy(
-            stage_out.at[part], w_out_new.at[layer, pl.ds(part * rows_out, rows_out)], sem_out.at[part])
+            rows = pl.ds(pl.multiple_of(part * rows_in, rows_in), rows_in)
+            return pltpu.make_async_copy(stage_in.at[part], w_in_new.at[layer, rows], sem_in.at[part])
+        rows = pl.ds(pl.multiple_of(part * rows_out, rows_out), rows_out)
+        return pltpu.make_async_copy(stage_out.at[part], w_out_new.at[layer, rows], sem_out.at[part])
 
     def pick(row, mat):
         at = lax.broadcasted_iota(jnp.int32, (1, LANE), 1) == mat
@@ -285,45 +287,66 @@
 
     def one_layer(layer, carry):
         scales(2 * layer, 0)
-        for part in range(parts):
+
+        def part_in(part, inner):
             @pl.when(layer > 0)
             def _():
                 out_copy(layer, 0, part).wait()
 
-            r0 = part * rows_in
-
-            def cols_in(j, inner):
-                cols = pl.ds(pl.multiple_of(j * LANE, LANE), LANE)
-                u = grad[2 * layer, r0:r0 + rows_in, cols] * pscale[r0:r0 + rows_in, :] * qscale[pl.ds(j, 1), :]
-                stage_in[part, :, cols] = wv_in[layer, r0:r0 + rows_in, cols] - u
-                return inner
-
-            lax.fori_loop(0, lch, cols_in, 0)
+            rows = pl.ds(pl.multiple_of(part * rows_in, rows_in), rows_in)
+
+            def cols_in(c, inner2):
+                p = pscale[rows, :]
+                for h in range(WCOLS // LANE):
+                    j = c * (WCOLS // LANE) + h
+                    cols = pl.ds(pl.multiple_of(j * LANE, LANE), LANE)
+                    u = grad[2 * layer, rows, cols] * p * qscale[pl.ds(j, 1), :]
+                    stage_in[part, :, cols] = wv_in[layer, rows, cols] - u
+                return inner2
+
+            lax.fori_loop(0, ml // WCOLS, cols_in, 0)
             out_copy(layer, 0, part).start()
-
+            return inner
+
+        lax.fori_loop(0, parts, part_in, 0)
         scales(2 * layer + 1, 1)
-        for part in range(parts):
+
+        def part_out(part, inner):
             @pl.when(layer > 0)
             def _():
                 out_copy(layer, 1, part).wait()
 
-            j0 = part * (rows_out // LANE)
-
-            def rows_loop(j, inner):
-                cols = pl.ds(pl.multiple_of((j0 + j) * LANE, LANE), LANE)
-                rows = pl.ds(pl.multiple_of(j * LANE, LANE), LANE)
-                u = grad[2 * layer + 1, :, cols] * pscale[...] * qscale[pl.ds(j0 + j, 1), :]
-                stage_out[part, rows, :] = wv_out[layer, cols, :] - u.T
-                return inner
-
-            lax.fori_loop(0, rows_out // LANE, rows_loop, 0)
+            p = pscale[...]
+            for h in range(rows_out // LANE):
+                j = part * (rows_out // LANE) + h
+                cols = pl.ds(pl.multiple_of(j * LANE, LANE), LANE)
+                u = grad[2 * layer + 1, :, cols] * p * qscale[pl.ds(j, 1), :]
+                stage_out[part, h * LANE:(h + 1) * LANE, :] = wv_out[layer, cols, :] - u.T
             out_copy(layer, 1, part).start()
+            return inner
+
+        lax.fori_loop(0, parts, part_out, 0)
+
+        @pl.when(layer == 0)
+        def _():
+            for each in range(layers):
+                for kind in range(2):
+                    mat = 2 * each + kind
+                    for j in range(sch):
+                        vec_s[kind, each:each + 1, j * LANE:(j + 1) * LANE] = short_new[mat, j:j + 1, :]
+                    for j in range(lch):
+                        vec_l[kind, each:each + 1, j * LANE:(j + 1) * LANE] = long_new[mat, j:j + 1, :]
+            for copy in vec_copies:
+                copy.start()
+
         return carry
 
     lax.fori_loop(0, layers, one_layer, 0)
     for kind in range(2):
         for part in range(parts):
             out_copy(layers - 1, kind, part).wait()
+    for copy in vec_copies:
+        copy.wait()
 
 
 def solution(mesh):
@@ -371,23 +394,26 @@
                 pltpu.SemaphoreType.DMA, pltpu.SemaphoreType.DMA,
             ],
             compiler_params=pltpu.CompilerParams(
-                collective_id=0, has_side_effects=True, vmem_limit_bytes=13 * 2 ** 20),
+                collective_id=0, has_side_effects=True, vmem_limit_bytes=22 * 2 ** 20),
             name='stats',
         )(*(pltpu.with_memory_space_constraint(item, pltpu.HBM) for item in (
             hyper_params, w_in, x_in, dy_in, row_in, col_in, w_out, x_out, dy_out, row_out, col_out)))
+        kept = tuple(pltpu.with_memory_space_constraint(item, pltpu.VMEM) for item in kept)
         parts = 4
         return pl.pallas_call(
             functools.partial(write_kernel, (layers, ms, ml, parts)),
             out_shape=tuple(jax.ShapeDtypeStruct(item.shape, F32) for item in (
                 w_in, row_in, col_in, w_out, row_out, col_out)),
             in_specs=[vmem_spec] * 6,
-            out_specs=(hbm_spec, vmem_spec, vmem_spec, hbm_spec, vmem_spec, vmem_spec),
+            out_specs=(hbm_spec,) * 6,
             scratch_shapes=[
                 pltpu.VMEM((parts, ms // parts, ml), F32), pltpu.VMEM((parts, ml // parts, ms), F32),
                 pltpu.VMEM((ms, LANE), F32), pltpu.VMEM((lch, LANE), F32),
+                pltpu.VMEM((2, layers, ms), F32), pltpu.VMEM((2, layers, ml), F32),
                 pltpu.SemaphoreType.DMA((parts,)), pltpu.SemaphoreType.DMA((parts,)),
+                pltpu.SemaphoreType.DMA((4,)),
             ],
-            compiler_params=pltpu.CompilerParams(vmem_limit_bytes=13 * 2 ** 20),
+            compiler_params=pltpu.CompilerParams(vmem_limit_bytes=22 * 2 ** 20),
             name='write',
         )(*kept)
 

time: 58.2 us -> 40.3 us (0.69)
  Pallas kernels: 57.4 us -> 39.6 us
    pallas_call x1, Pallas kernels: 41.1 us -> 29.6 us  [local_step(): pl.pallas_call(functools.partial(stats_kernel, dims), out_shape=(pltpu.VM...]
    pallas_call x1, Pallas kernels: 16.3 us -> 9.97 us  [local_step(): pl.pallas_call(functools.partial(write_kernel, (layers, ms, ml, parts)),...]
where the time goes in v2:
time: 40.3 us; the launch traced here: 40.2 us
  Pallas kernels  39.6 us (98%)
  between operations  0.64 us (2%)
    pallas_call x1, Pallas kernels, local_step(): pl.pallas_call(functools.partial(stats_kernel, dims), out_shape=(pltpu.VM...  29.6 us
    pallas_call x1, Pallas kernels, local_step(): pl.pallas_call(functools.partial(write_kernel, (layers, ms, ml, parts)),...  9.97 us

profile of v2, /device:TPU:0, one launch (start us, length us, event | category | flops | bytes accessed | tf_op | source)
XLA Modules:
  0.0 40.2 jit_solution(15507429029840057767)
XLA Ops:
  0.6 29.6 %stats.1 = (f32[8,256,2560]{2,1,0:T(8,128)S(1)}, f32[4,256,2560]{2,1,0:T(8,128)S(1)}, f32[4,2560,256]{2,1,0:T(8,128)S(1)}, f32[8,2,128]{2,1,0:T(2,128)S(1)}, f32...) custom-call(f32[3]{0:T(128)} %hyper_hbm.1, f32[4,256,2560]{2,1,0:T(8,128)} %w_in.1, bf16[4,512,256]{2,1,0:T(8,128)(2,1)} %x_in.1, ...), custom_call_target="tpu_custom_call" | custom-call | tf_op jit(solution)/shard_map/stats/pallas_call | solution.py:373
  30.2 10.0 %write.1 = (f32[4,256,2560]{2,1,0:T(8,128)}, f32[4,256]{1,0:T(4,128)}, f32[4,2560]{1,0:T(4,128)}, f32[4,2560,256]{2,1,0:T(8,128)}, f32[4,2560]{1,0:T(4,128)}, /*index=5*/f32[4,256]{1,0:T(4,128)}) custom-call(f32[8,256,2560]{2,1,0:T(8,128)S(1)} %get-tuple-element.12.grad, f32[4,256,2560]{2,1,0:T(8,128)S(1)} %get-tuple-element.13.wv_in, ...), custom_call_target="tpu_custom_call" | custom-call | tf_op jit(solution)/shard_map/write/pallas_call | solution.py:403

commit v3 on v0

v3 whole, which is shorter than its diff:
```python
import functools

import jax
import jax.numpy as jnp
from jax import lax
from jax.experimental import pallas as pl
from jax.experimental.pallas import tpu as pltpu
from jax.sharding import PartitionSpec as P

EPS_ONE = 1e-30
EPS_TWO = 1e-3
LANE = 128
CHUNK = 1280
MESH = pl.DeviceIdType.MESH
F32 = jnp.float32
VMEM_GRANT = 20 * 2 ** 20


def tree(items):
    while len(items) > 1:
        items = [items[k] + items[k + 1] if k + 1 < len(items) else items[k] for k in range(0, len(items), 2)]
    return items[0]


def total(value):
    return jnp.sum(jnp.sum(value, axis=1, keepdims=True), axis=0, keepdims=True)


def stats_kernel(dims, hyper_hbm, w_in, x_in, dy_in, row_in, col_in, w_out, x_out, dy_out, row_out, col_out,
                 grad_lo, grad_hi, wv_in, wv_out, short_new, long_new, short_scale, long_scale, step_size,
                 act_s, act_l, lhs_t, old_s_in, old_l_in, old_s_out, old_l_out, short_old, long_old,
                 long_buf, short_buf, upd_buf, wsq_buf, racc, cacc, linv, pack, wpack, hyper_ref,
                 act_sem, w_sem, old_sem, long_send, long_recv, short_send, short_recv, fin_send, fin_recv):
    n_col, n_row, layers, ms, ml, d_model, d_hidden = dims
    n_dev = n_col * n_row
    half = layers // 2
    sch, lch = ms // LANE, ml // LANE
    my_col = lax.axis_index('col')
    my_row = lax.axis_index('row')
    me = my_col * n_row + my_row

    def act_copies(layer, kind):
        slot = 2 * lax.rem(layer, 2) + kind
        src_s = (x_in, dy_out)[kind]
        src_l = (dy_in, x_out)[kind]
        return (pltpu.make_async_copy(src_s.at[layer], act_s.at[slot], act_sem.at[slot, 0]),
                pltpu.make_async_copy(src_l.at[layer], act_l.at[slot], act_sem.at[slot, 1]))

    def w_copy(layer, kind):
        src = (w_in, w_out)[kind]
        dst = (wv_in, wv_out)[kind]
        return pltpu.make_async_copy(src.at[layer], dst.at[layer], w_sem.at[layer, kind])

    old_copies = [pltpu.make_async_copy(src, dst, old_sem.at[idx]) for idx, (src, dst) in enumerate(
        ((row_in, old_s_in), (col_in, old_l_in), (col_out, old_s_out), (row_out, old_l_out), (hyper_hbm, hyper_ref)))]

    for layer in range(2):
        for kind in range(2):
            for copy in act_copies(layer, kind):
                copy.start()
    for copy in old_copies:
        copy.start()

    barrier = pltpu.get_barrier_semaphore()

    def peer_of(step):
        lin = lax.rem(me + step, n_dev)
        return (lin // n_row, lax.rem(lin, n_row))

    for step in range(1, n_dev):
        pl.semaphore_signal(barrier, inc=1, device_id=peer_of(step), device_id_type=MESH)

    pack[...] = jnp.zeros_like(pack)
    wpack[...] = jnp.zeros_like(wpack)

    def long_copy(mat, step):
        peer = lax.rem(my_row + step, n_row)
        return pltpu.make_async_remote_copy(
            src_ref=long_buf.at[mat, my_row], dst_ref=long_buf.at[mat, my_row],
            send_sem=long_send.at[mat], recv_sem=long_recv.at[mat],
            device_id=(my_col, peer), device_id_type=MESH)

    def short_copy(mat):
        return pltpu.make_async_remote_copy(
            src_ref=short_buf.at[mat, my_col], dst_ref=short_buf.at[mat, my_col],
            send_sem=short_send.at[mat], recv_sem=short_recv.at[mat],
            device_id=(n_col - 1 - my_col, my_row), device_id_type=MESH)

    def long_others(mat, sem):
        ref = long_buf.at[mat, pl.ds(0, n_row - 1)]
        return pltpu.make_async_copy(ref, ref, sem.at[mat])

    def fin_copy(buf, idx, step):
        return pltpu.make_async_remote_copy(
            src_ref=buf.at[me], dst_ref=buf.at[me], send_sem=fin_send.at[idx], recv_sem=fin_recv.at[idx],
            device_id=peer_of(step), device_id_type=MESH)

    def fin_others(buf, sem):
        ref = buf.at[pl.ds(0, n_dev - 1)]
        return pltpu.make_async_copy(ref, ref, sem)

    def put(where, lane, value):
        at = lax.broadcasted_iota(jnp.int32, (1, LANE), 1) == lane
        where[...] += jnp.where(at, value, 0.0)

    def dot_part(grad, base, mat, slot, c):
        cols = slice(c * CHUNK, (c + 1) * CHUNK)
        g = jnp.dot(lhs_t[...], act_l[slot, :, cols], preferred_element_type=F32)
        grad[mat - base, :, cols] = g
        sq = g * g
        part = tree([sq[:, j * LANE:(j + 1) * LANE] for j in range(CHUNK // LANE)])
        if c == 0:
            racc[...] = part
        else:
            racc[...] += part
        cacc[:, cols] = jnp.sum(sq.reshape(ms // 8, 8, CHUNK), axis=0)

    def upd_part(grad, base, mat, c):
        scale = short_scale[mat]
        acc = []
        for j in range(c * CHUNK // LANE, (c + 1) * CHUNK // LANE):
            u = grad[mat - base, :, j * LANE:(j + 1) * LANE] * scale
            acc.append(jnp.sum((u * u).reshape(ms // 8, 8, LANE), axis=0) * linv[j:j + 1, :])
        return tree(acc)

    def stats(layer, kind):
        mat = 2 * layer + kind
        long_others(mat, long_recv).wait()
        short_copy(mat).wait_recv()
        beta_two = hyper_ref[0]
        lsum = tree([long_buf[mat, dev] for dev in range(n_row)])
        ssum = tree([short_buf[mat, dev] for dev in range(n_col)])
        lnew = beta_two * long_old[mat] + (1.0 - beta_two) * (lsum * (1.0 / d_model) + EPS_ONE)
        snew = beta_two * short_old[mat] + (1.0 - beta_two) * (ssum * (1.0 / d_hidden) + EPS_ONE)
        long_new[mat] = lnew
        short_new[mat] = snew
        if kind == 0:
            rho = total(snew)
            rs = lax.rsqrt(snew / (rho * (1.0 / ms)))
            rl = lax.rsqrt(lnew)
        else:
            rho = total(lnew)
            rs = lax.rsqrt(snew)
            rl = lax.rsqrt(lnew / (rho * (1.0 / ml)))
        long_scale[mat] = rl
        linv[...] = rl * rl
        for j in range(sch):
            short_scale[mat, j * LANE:(j + 1) * LANE, :] = jnp.broadcast_to(rs[j:j + 1, :], (LANE, LANE)).T
        put(pack, mat + 2 * layers, rho)

    def send(mat):
        for j in range(lch):
            long_buf[mat, my_row, j:j + 1, :] = jnp.sum(cacc[:, j * LANE:(j + 1) * LANE], axis=0, keepdims=True)
        for j in range(sch):
            part = racc[j * LANE:(j + 1) * LANE, :].T
            short_buf[mat, my_col, j:j + 1, :] = jnp.sum(part, axis=0, keepdims=True)
        for step in range(1, n_row):
            long_copy(mat, step).start()
        short_copy(mat).start()

    def form_layer(layer, with_upd):
        for kind in range(2):
            mat = 2 * layer + kind
            slot = 2 * lax.rem(layer, 2) + kind
            for copy in act_copies(layer, kind):
                copy.wait()
            if with_upd:
                stats(layer - half, kind)
            lhs_t[...] = act_s[slot].T
            acc = []
            for c in range(ml // CHUNK):
                if with_upd:
                    acc.append(upd_part(grad_lo, 0, mat - 2 * half, c))
                dot_part(*((grad_hi, 2 * half) if with_upd else (grad_lo, 0)), mat, slot, c)
            if with_upd:
                put(pack, mat - 2 * half, total(tree(acc)))
            else:
                for copy in act_copies(layer + half, kind):
                    copy.start()
            w_copy(layer, kind).start()
            send(mat)

    def first_half(layer, carry):
        form_layer(layer, False)

        @pl.when(layer == 0)
        def _():
            for copy in old_copies:
                copy.wait()
            for kind, (src_s, src_l) in enumerate(((old_s_in, old_l_in), (old_s_out, old_l_out))):
                for each in range(layers):
                    for j in range(sch):
                        short_old[2 * each + kind, j:j + 1, :] = src_s[each:each + 1, j * LANE:(j + 1) * LANE]
                    for j in range(lch):
                        long_old[2 * each + kind, j:j + 1, :] = src_l[each:each + 1, j * LANE:(j + 1) * LANE]

        return carry

    def second_half(layer, carry):
        form_layer(layer, True)
        return carry

    def upd_tail(layer, carry):
        for kind in range(2):
            mat = 2 * layer + kind
            stats(layer, kind)
            put(pack, mat, total(tree([upd_part(grad_hi, 2 * half, mat, c) for c in range(ml // CHUNK)])))
        return carry

    pl.semaphore_wait(barrier, n_dev - 1)
    lax.fori_loop(0, half, first_half, 0)
    lax.fori_loop(half, layers, second_half, 0)
    lax.fori_loop(half, layers, upd_tail, 0)

    upd_buf[me] = pack[...]
    for step in range(1, n_dev):
        fin_copy(upd_buf, 0, step).start()

    def weight_sq(layer, kind):
        w_copy(layer, kind).wait()
        ref = (wv_in, wv_out)[kind]
        rows, cols = ref.shape[1:]
        block = max(8, 8 * 8 * 20 * LANE // cols)

        def chunk(t, acc):
            v = ref[layer, pl.ds(pl.multiple_of(t * block, 8), block), :]
            v = v * v
            part = tree([v[:, j * LANE:(j + 1) * LANE] for j in range(cols // LANE)])
            return acc + tree([part[8 * j:8 * j + 8] for j in range(block // 8)])

        acc = lax.fori_loop(0, rows // block, chunk, jnp.zeros((8, LANE), F32))
        put(wpack, 2 * layer + kind, total(acc))

    def weights(layer, carry):
        for kind in range(2):
            weight_sq(layer, kind)
        return carry

    lax.fori_loop(0, layers, weights, 0)
    wsq_buf[me] = wpack[...]
    for step in range(1, n_dev):
        fin_copy(wsq_buf, 1, step).start()

    for mat in range(2 * layers):
        long_others(mat, long_send).wait()
        short_copy(mat).wait_send()
    fin_others(upd_buf, fin_send.at[0]).wait()
    fin_others(upd_buf, fin_recv.at[0]).wait()
    lane = lax.broadcasted_iota(jnp.int32, (1, LANE), 1)
    is_in = lax.rem(lane, 2) == 0
    valid = lane < 2 * layers
    shift = LANE - 2 * layers
    rho_sum = pltpu.roll(tree([upd_buf[dev] for dev in range(n_dev)]), shift, 1)
    row_mean = rho_sum * jnp.where(is_in, 1.0 / (n_col * d_model), 1.0 / (n_row * d_hidden))
    row_mean = jnp.where(valid, row_mean, 1.0)
    per_block = jnp.where(is_in, 1.0 / ms, 1.0 / ml)

    def ratio(rho):
        return row_mean / jnp.where(valid, pltpu.roll(rho, shift, 1) * per_block, 1.0)

    upd_sq = tree([upd_buf[dev] * ratio(upd_buf[dev]) for dev in range(n_dev)])
    n_total = float(d_model * d_hidden)
    upd_rms = jnp.sqrt(jnp.where(valid, upd_sq, 0.0) * (1.0 / n_total))
    before_w = hyper_ref[1] * jnp.sqrt(ratio(pack[...])) / jnp.maximum(1.0, upd_rms / hyper_ref[2])

    fin_others(wsq_buf, fin_send.at[1]).wait()
    fin_others(wsq_buf, fin_recv.at[1]).wait()
    w_sq = tree([wsq_buf[dev] for dev in range(n_dev)])
    w_rms = jnp.sqrt(w_sq * (1.0 / n_total))
    size = before_w * jnp.maximum(EPS_TWO, w_rms)
    step_size[...] = jnp.broadcast_to(size, (LANE, LANE)).T[:2 * layers, :]


def write_kernel(dims, grad_lo, grad_hi, wv_in, wv_out, short_new, long_new, short_scale, long_scale, step_size,
                 w_in_new, row_in_new, col_in_new, w_out_new, row_out_new, col_out_new,
                 stage_in, stage_out, vec_s, vec_l, sem_in, sem_out, sem_vec):
    layers, ms, ml, parts = dims
    half = layers // 2
    sch, lch = ms // LANE, ml // LANE
    rows_in, rows_out = ms // parts, ml // parts

    vec_copies = [pltpu.make_async_copy(src, dst, sem_vec.at[idx]) for idx, (src, dst) in enumerate(
        ((vec_s.at[0], row_in_new), (vec_l.at[0], col_in_new), (vec_s.at[1], col_out_new), (vec_l.at[1], row_out_new)))]

    def out_copy(layer, kind, part):
        if kind == 0:
            rows = pl.ds(pl.multiple_of(part * rows_in, rows_in), rows_in)
            return pltpu.make_async_copy(stage_in.at[part], w_in_new.at[layer, rows], sem_in.at[part])
        rows = pl.ds(pl.multiple_of(part * rows_out, rows_out), rows_out)
        return pltpu.make_async_copy(stage_out.at[part], w_out_new.at[layer, rows], sem_out.at[part])

    def one_part(layer, grad, mat, part):
        @pl.when(layer > 0)
        def _():
            for kind in range(2):
                out_copy(layer, kind, part).wait()

        rows = pl.ds(pl.multiple_of(part * rows_in, rows_in), rows_in)
        p_out = short_scale[2 * layer + 1] * step_size[pl.ds(2 * layer + 1, 1), :]
        p_in = short_scale[2 * layer, rows, :] * step_size[pl.ds(2 * layer, 1), :]
        per_row = rows_out // LANE
        for h in range(per_row):
            j = part * per_row + h
            cols = pl.ds(pl.multiple_of(j * LANE, LANE), LANE)
            u = grad[mat + 1, :, cols] * p_out * long_scale[2 * layer + 1, pl.ds(j, 1), :]
            stage_out[part, h * LANE:(h + 1) * LANE, :] = wv_out[layer, cols, :] - u.T
            for j in range(h * (lch // per_row), (h + 1) * (lch // per_row)):
                cols = slice(j * LANE, (j + 1) * LANE)
                u = grad[mat, rows, cols] * p_in * long_scale[2 * layer, j:j + 1, :]
                stage_in[part, :, cols] = wv_in[layer, rows, cols] - u
        for kind in range(2):
            out_copy(layer, kind, part).start()

    def loop(base, grad):
        def one(t, carry):
            layer = base + t // parts
            one_part(layer, grad, 2 * (t // parts), lax.rem(t, parts))
            return carry

        lax.fori_loop(0, half * parts, one, 0)

    loop(0, grad_lo)
    for each in range(layers):
        for kind in range(2):
            mat = 2 * each + kind
            for j in range(sch):
                vec_s[kind, each:each + 1, j * LANE:(j + 1) * LANE] = short_new[mat, j:j + 1, :]
            for j in range(lch):
                vec_l[kind, each:each + 1, j * LANE:(j + 1) * LANE] = long_new[mat, j:j + 1, :]
    for copy in vec_copies:
        copy.start()
    loop(half, grad_hi)
    for kind in range(2):
        for part in range(parts):
            out_copy(layers - 1, kind, part).wait()
    for copy in vec_copies:
        copy.wait()


def solution(mesh):
    n_col = mesh.shape['col']
    n_row = mesh.shape['row']
    tile_in = P(None, 'row', 'col')
    tile_out = P(None, 'col', 'row')
    lane_row = P(None, None, 'row')
    lane_col = P(None, None, 'col')
    vec_row = P(None, 'row')
    vec_col = P(None, 'col')

    def local_step(hyper_params, w_in, x_in, dy_in, row_in, col_in, w_out, x_out, dy_out, row_out, col_out):
        layers, ms, ml = w_in.shape
        tokens = x_in.shape[1]
        mats = 2 * layers
        sch, lch = ms // LANE, ml // LANE
        n_dev = n_col * n_row
        d_model, d_hidden = ms * n_row, ml * n_col
        hbm_spec = pl.BlockSpec(memory_space=pltpu.HBM)
        vmem_spec = pl.BlockSpec(memory_space=pltpu.VMEM)
        dims = (n_col, n_row, layers, ms, ml, d_model, d_hidden)
        bf16 = jnp.bfloat16
        dma = pltpu.SemaphoreType.DMA
        kept = pl.pallas_call(
            functools.partial(stats_kernel, dims),
            out_shape=(pltpu.VMEM((layers, ms, ml), F32), pltpu.VMEM((layers, ms, ml), F32),
                       pltpu.VMEM((layers, ms, ml), F32), pltpu.VMEM((layers, ml, ms), F32),
                       pltpu.VMEM((mats, sch, LANE), F32), pltpu.VMEM((mats, lch, LANE), F32),
                       pltpu.VMEM((mats, ms, LANE), F32), pltpu.VMEM((mats, lch, LANE), F32),
                       pltpu.VMEM((mats, LANE), F32)),
            in_specs=[hbm_spec] * 11,
            out_specs=(vmem_spec,) * 9,
            scratch_shapes=[
                pltpu.VMEM((4, tokens, ms), bf16), pltpu.VMEM((4, tokens, ml), bf16),
                pltpu.VMEM((ms, tokens), bf16),
                pltpu.VMEM((layers, ms), F32), pltpu.VMEM((layers, ml), F32),
                pltpu.VMEM((layers, ms), F32), pltpu.VMEM((layers, ml), F32),
                pltpu.VMEM((mats, sch, LANE), F32), pltpu.VMEM((mats, lch, LANE), F32),
                pltpu.VMEM((mats, n_row, lch, LANE), F32), pltpu.VMEM((mats, n_col, sch, LANE), F32),
                pltpu.VMEM((n_dev, 1, LANE), F32), pltpu.VMEM((n_dev, 1, LANE), F32),
                pltpu.VMEM((ms, LANE), F32), pltpu.VMEM((8, ml), F32),
                pltpu.VMEM((lch, LANE), F32), pltpu.VMEM((1, LANE), F32), pltpu.VMEM((1, LANE), F32),
                pltpu.SMEM((3,), F32),
                dma((4, 2)), dma((layers, 2)), dma((5,)),
                dma((mats,)), dma((mats,)), dma((mats,)), dma((mats,)), dma((2,)), dma((2,)),
            ],
            compiler_params=pltpu.CompilerParams(
                collective_id=0, has_side_effects=True, vmem_limit_bytes=VMEM_GRANT),
            name='stats',
        )(*(pltpu.with_memory_space_constraint(item, pltpu.HBM) for item in (
            hyper_params, w_in, x_in, dy_in, row_in, col_in, w_out, x_out, dy_out, row_out, col_out)))
        kept = tuple(pltpu.with_memory_space_constraint(item, pltpu.VMEM) for item in kept)
        parts = 4
        return pl.pallas_call(
            functools.partial(write_kernel, (layers, ms, ml, parts)),
            out_shape=tuple(jax.ShapeDtypeStruct(item.shape, F32) for item in (
                w_in, row_in, col_in, w_out, row_out, col_out)),
            in_specs=[vmem_spec] * 9,
            out_specs=(hbm_spec,) * 6,
            scratch_shapes=[
                pltpu.VMEM((parts, ms // parts, ml), F32), pltpu.VMEM((parts, ml // parts, ms), F32),
                pltpu.VMEM((2, layers, ms), F32), pltpu.VMEM((2, layers, ml), F32),
                dma((parts,)), dma((parts,)), dma((4,)),
            ],
            compiler_params=pltpu.CompilerParams(vmem_limit_bytes=VMEM_GRANT),
            name='write',
        )(*kept)

    return jax.shard_map(local_step, mesh=mesh, in_specs=(P(), tile_in, lane_row, lane_col, vec_row, vec_col, tile_out, lane_col, lane_row, vec_col, vec_row), out_specs=(tile_in, vec_row, vec_col, tile_out, vec_col, vec_row), check_vma=False)
```

time: 243 us -> 33.3 us (0.14)
  other arithmetic: 75.5 us -> 0 us
  blocking collectives: 73.4 us -> 0 us
  between operations: 55.8 us -> 0.64 us
  Pallas kernels: 0 us -> 32.5 us
  matrix products: 29.1 us -> 0 us
  local copies, waits for them, and re-layouts: 7.21 us -> 0 us
    psum x3 -> x0, blocking collectives: 73.4 us -> none  [the longest x1 34.9 us: update_block(): scalar_sum = lax.psum(scalars, BOTH_AXES)]
    another operation x18 -> x0, other arithmetic: 41.4 us -> none  [the longest x10 30.8 us: local_step(): jnp.stack([res_item[out_idx] for res_item in results])]
    pallas_call x0 -> x2, Pallas kernels: none -> 32.5 us  [the longest x1 25.1 us: local_step(): pl.pallas_call(functools.partial(stats_kernel, dims), out_shape=(pltpu.VM...]
    dot_general x8 -> x0, matrix products: 29.1 us -> none  [update_block(): lax.dot_general(x_blk, dy_blk, (((0,), (0,)), ((), ())), preferred_elemen...]
    reduce_sum x10 -> x0, other arithmetic: 26.2 us -> none  [the longest x8 14.9 us: update_block(): upd_sq = lax.psum(jnp.sum(update * update), BOTH_AXES)]
    slice x9 -> x0, local copies, waits for them, and re-layouts: 5.6 us -> none  [the longest x7 4.42 us: update_block(): w_rms = jnp.sqrt(scalar_sum[1] / n_total)]
    add x8 -> x0, other arithmetic: 2.88 us -> none  [update_block(): col_new = beta_two * col_old + (1.0 - beta_two) * (col_sum / n_rows)]
    mul x2 -> x0, other arithmetic: 2.62 us -> none  [the longest x1 1.37 us: update_block(): row_new = beta_two * row_old + (1.0 - beta_two) * (row_sum / n_cols)]
  transfers between devices with their start and end apart: 1 -> 0, of which waited for: 0 -> 0; matrix products, arithmetic and copies ran while one was open for 13% -> 0% of each run, Pallas kernels for 0% -> 0%
where the time goes in v3:
time: 33.3 us; the launch traced here: 33.2 us
  Pallas kernels  32.5 us (98%)
  between operations  0.64 us (2%)
    pallas_call x1, Pallas kernels, local_step(): pl.pallas_call(functools.partial(stats_kernel, dims), out_shape=(pltpu.VM...  25.1 us
    pallas_call x1, Pallas kernels, local_step(): pl.pallas_call(functools.partial(write_kernel, (layers, ms, ml, parts)),...  7.45 us

profile of v3, /device:TPU:0, one launch (start us, length us, event | category | flops | bytes accessed | tf_op | source)
XLA Modules:
  0.0 33.2 jit_solution(16284170494519779684)
XLA Ops:
  0.6 25.1 %stats.1 = (f32[4,256,2560]{2,1,0:T(8,128)S(1)}, f32[4,256,2560]{2,1,0:T(8,128)S(1)}, f32[4,256,2560]{2,1,0:T(8,128)S(1)}, f32[4,2560,256]{2,1,0:T(8,128)S(1)}, ...) custom-call(f32[3]{0:T(128)} %hyper_hbm.1, ...), custom_call_target="tpu_custom_call" | custom-call | tf_op jit(solution)/shard_map/stats/pallas_call | solution.py:362
  25.7 7.5 %write.1 = (f32[4,256,2560]{2,1,0:T(8,128)}, f32[4,256]{1,0:T(4,128)}, f32[4,2560]{1,0:T(4,128)}, f32[4,2560,256]{2,1,0:T(8,128)}, f32[4,2560]{1,0:T(4,128)}, /*index=5*/f32[4,256]{1,0:T(4,128)}) custom-call(f32[4,256,2560]{2,1,0:T(8,128)S(1)} %get-tuple-element.15.grad_lo, f32[4,256,2560]{2,1,0:T(8,128)S(1)} %get-tuple-element.16.grad_hi, ...), custom_call_target="tpu_custom_call" | custom-call | tf_op jit(solution)/shard_map/write/pallas_call | solution.py:392

commit v4 on v3

--- a/solution.py
+++ b/solution.py
@@ -11,6 +11,7 @@
 EPS_TWO = 1e-3
 LANE = 128
 CHUNK = 1280
+WSTEPS = 8
 MESH = pl.DeviceIdType.MESH
 F32 = jnp.float32
 VMEM_GRANT = 20 * 2 ** 20
@@ -60,6 +61,9 @@
                 copy.start()
     for copy in old_copies:
         copy.start()
+    for layer in range(layers):
+        for kind in range(2):
+            w_copy(layer, kind).start(priority=1)
 
     barrier = pltpu.get_barrier_semaphore()
 
@@ -116,12 +120,13 @@
         cacc[:, cols] = jnp.sum(sq.reshape(ms // 8, 8, CHUNK), axis=0)
 
     def upd_part(grad, base, mat, c):
-        scale = short_scale[mat]
-        acc = []
-        for j in range(c * CHUNK // LANE, (c + 1) * CHUNK // LANE):
-            u = grad[mat - base, :, j * LANE:(j + 1) * LANE] * scale
-            acc.append(jnp.sum((u * u).reshape(ms // 8, 8, LANE), axis=0) * linv[j:j + 1, :])
-        return tree(acc)
+        cols = slice(c * CHUNK, (c + 1) * CHUNK)
+        acc = jnp.zeros((8, CHUNK), F32)
+        for r in range(0, ms, 8):
+            u = grad[mat - base, r:r + 8, cols] * jnp.tile(short_scale[mat, r:r + 8, :], (1, CHUNK // LANE))
+            acc = acc + u * u
+        first = c * CHUNK // LANE
+        return tree([acc[:, j * LANE:(j + 1) * LANE] * linv[first + j:first + j + 1, :] for j in range(CHUNK // LANE)])
 
     def stats(layer, kind):
         mat = 2 * layer + kind
@@ -177,7 +182,11 @@
             else:
                 for copy in act_copies(layer + half, kind):
                     copy.start()
-            w_copy(layer, kind).start()
+            if kind == 0 and not with_upd:
+                @pl.when(layer == 0)
+                def _():
+                    pl.semaphore_wait(barrier, n_dev - 1)
+
             send(mat)
 
     def first_half(layer, carry):
@@ -207,36 +216,40 @@
             put(pack, mat, total(tree([upd_part(grad_hi, 2 * half, mat, c) for c in range(ml // CHUNK)])))
         return carry
 
-    pl.semaphore_wait(barrier, n_dev - 1)
     lax.fori_loop(0, half, first_half, 0)
     lax.fori_loop(half, layers, second_half, 0)
-    lax.fori_loop(half, layers, upd_tail, 0)
-
-    upd_buf[me] = pack[...]
-    for step in range(1, n_dev):
-        fin_copy(upd_buf, 0, step).start()
-
     def weight_sq(layer, kind):
         w_copy(layer, kind).wait()
         ref = (wv_in, wv_out)[kind]
         rows, cols = ref.shape[1:]
-        block = max(8, 8 * 8 * 20 * LANE // cols)
+        slab = max(8, 80 * LANE // cols // 8 * 8)
+        width = min(cols, 10 * LANE)
+        trip = WSTEPS * slab
 
         def chunk(t, acc):
-            v = ref[layer, pl.ds(pl.multiple_of(t * block, 8), block), :]
-            v = v * v
-            part = tree([v[:, j * LANE:(j + 1) * LANE] for j in range(cols // LANE)])
-            return acc + tree([part[8 * j:8 * j + 8] for j in range(block // 8)])
-
-        acc = lax.fori_loop(0, rows // block, chunk, jnp.zeros((8, LANE), F32))
-        put(wpack, 2 * layer + kind, total(acc))
+            for step in range(WSTEPS):
+                at = pl.ds(pl.multiple_of(t * trip + step * slab, 8), slab)
+                for c in range(0, cols, width):
+                    v = ref[layer, at, c:c + width]
+                    acc = acc + v * v
+            return acc
+
+        acc = lax.fori_loop(0, rows // trip, chunk, jnp.zeros((slab, width), F32))
+        acc = tree([acc[:, j * LANE:(j + 1) * LANE] for j in range(width // LANE)])
+        put(wpack, 2 * layer + kind, total(tree([acc[j:j + 8] for j in range(0, slab, 8)])))
 
     def weights(layer, carry):
         for kind in range(2):
             weight_sq(layer, kind)
         return carry
 
-    lax.fori_loop(0, layers, weights, 0)
+    lax.fori_loop(0, layers - 1, weights, 0)
+    lax.fori_loop(half, layers, upd_tail, 0)
+    upd_buf[me] = pack[...]
+    for step in range(1, n_dev):
+        fin_copy(upd_buf, 0, step).start()
+
+    lax.fori_loop(layers - 1, layers, weights, 0)
     wsq_buf[me] = wpack[...]
     for step in range(1, n_dev):
         fin_copy(wsq_buf, 1, step).start()

time: 33.3 us -> 30.7 us (0.922)
  Pallas kernels: 32.5 us -> 29.9 us
    pallas_call x1, Pallas kernels: 25.1 us -> 22.5 us  [local_step(): pl.pallas_call(functools.partial(stats_kernel, dims), out_shape=(pltpu.VM...]
where the time goes in v4:
time: 30.7 us; the launch traced here: 30.6 us
  Pallas kernels  29.9 us (97%)
  between operations  0.64 us (2%)
    pallas_call x1, Pallas kernels, local_step(): pl.pallas_call(functools.partial(stats_kernel, dims), out_shape=(pltpu.VM...  22.5 us
    pallas_call x1, Pallas kernels, local_step(): pl.pallas_call(functools.partial(write_kernel, (layers, ms, ml, parts)),...  7.45 us

profile of v4, /device:TPU:0, one launch (start us, length us, event | category | flops | bytes accessed | tf_op | source)
XLA Modules:
  0.0 30.6 jit_solution(17829428251078965659)
XLA Ops:
  0.6 22.5 %stats.1 = (f32[4,256,2560]{2,1,0:T(8,128)S(1)}, f32[4,256,2560]{2,1,0:T(8,128)S(1)}, f32[4,256,2560]{2,1,0:T(8,128)S(1)}, f32[4,2560,256]{2,1,0:T(8,128)S(1)}, ...) custom-call(f32[3]{0:T(128)} %hyper_hbm.1, ...), custom_call_target="tpu_custom_call" | custom-call | tf_op jit(solution)/shard_map/stats/pallas_call | solution.py:375
  23.1 7.5 %write.1 = (f32[4,256,2560]{2,1,0:T(8,128)}, f32[4,256]{1,0:T(4,128)}, f32[4,2560]{1,0:T(4,128)}, f32[4,2560,256]{2,1,0:T(8,128)}, f32[4,2560]{1,0:T(4,128)}, /*index=5*/f32[4,256]{1,0:T(4,128)}) custom-call(f32[4,256,2560]{2,1,0:T(8,128)S(1)} %get-tuple-element.15.grad_lo, f32[4,256,2560]{2,1,0:T(8,128)S(1)} %get-tuple-element.16.grad_hi, ...), custom_call_target="tpu_custom_call" | custom-call | tf_op jit(solution)/shard_map/write/pallas_call | solution.py:405

commit v5 on v4

--- a/solution.py
+++ b/solution.py
@@ -11,7 +11,7 @@
 EPS_TWO = 1e-3
 LANE = 128
 CHUNK = 1280
-WSTEPS = 8
+WSTEPS = 32
 MESH = pl.DeviceIdType.MESH
 F32 = jnp.float32
 VMEM_GRANT = 20 * 2 ** 20
@@ -44,8 +44,12 @@
         slot = 2 * lax.rem(layer, 2) + kind
         src_s = (x_in, dy_out)[kind]
         src_l = (dy_in, x_out)[kind]
-        return (pltpu.make_async_copy(src_s.at[layer], act_s.at[slot], act_sem.at[slot, 0]),
-                pltpu.make_async_copy(src_l.at[layer], act_l.at[slot], act_sem.at[slot, 1]))
+        copies = [pltpu.make_async_copy(src_s.at[layer], act_s.at[slot], act_sem.at[slot, 0])]
+        for c in range(ml // CHUNK):
+            cols = pl.ds(c * CHUNK, CHUNK)
+            copies.append(pltpu.make_async_copy(
+                src_l.at[layer, :, cols], act_l.at[slot, :, cols], act_sem.at[slot, 1 + c]))
+        return copies
 
     def w_copy(layer, kind):
         src = (w_in, w_out)[kind]
@@ -163,17 +167,21 @@
             long_copy(mat, step).start()
         short_copy(mat).start()
 
-    def form_layer(layer, with_upd):
+    def form_layer(layer, with_upd, layer_is_first=False):
         for kind in range(2):
             mat = 2 * layer + kind
             slot = 2 * lax.rem(layer, 2) + kind
-            for copy in act_copies(layer, kind):
+            copies = act_copies(layer, kind)
+            early = layer_is_first and kind == 0
+            for copy in copies[:2] if early else copies:
                 copy.wait()
             if with_upd:
                 stats(layer - half, kind)
             lhs_t[...] = act_s[slot].T
             acc = []
             for c in range(ml // CHUNK):
+                if c and early:
+                    copies[1 + c].wait()
                 if with_upd:
                     acc.append(upd_part(grad_lo, 0, mat - 2 * half, c))
                 dot_part(*((grad_hi, 2 * half) if with_upd else (grad_lo, 0)), mat, slot, c)
@@ -182,27 +190,22 @@
             else:
                 for copy in act_copies(layer + half, kind):
                     copy.start()
-            if kind == 0 and not with_upd:
-                @pl.when(layer == 0)
-                def _():
-                    pl.semaphore_wait(barrier, n_dev - 1)
-
+            if early:
+                pl.semaphore_wait(barrier, n_dev - 1)
             send(mat)
+
+    def spread_old():
+        for copy in old_copies:
+            copy.wait()
+        for kind, (src_s, src_l) in enumerate(((old_s_in, old_l_in), (old_s_out, old_l_out))):
+            for each in range(layers):
+                for j in range(sch):
+                    short_old[2 * each + kind, j:j + 1, :] = src_s[each:each + 1, j * LANE:(j + 1) * LANE]
+                for j in range(lch):
+                    long_old[2 * each + kind, j:j + 1, :] = src_l[each:each + 1, j * LANE:(j + 1) * LANE]
 
     def first_half(layer, carry):
         form_layer(layer, False)
-
-        @pl.when(layer == 0)
-        def _():
-            for copy in old_copies:
-                copy.wait()
-            for kind, (src_s, src_l) in enumerate(((old_s_in, old_l_in), (old_s_out, old_l_out))):
-                for each in range(layers):
-                    for j in range(sch):
-                        short_old[2 * each + kind, j:j + 1, :] = src_s[each:each + 1, j * LANE:(j + 1) * LANE]
-                    for j in range(lch):
-                        long_old[2 * each + kind, j:j + 1, :] = src_l[each:each + 1, j * LANE:(j + 1) * LANE]
-
         return carry
 
     def second_half(layer, carry):
@@ -216,8 +219,6 @@
             put(pack, mat, total(tree([upd_part(grad_hi, 2 * half, mat, c) for c in range(ml // CHUNK)])))
         return carry
 
-    lax.fori_loop(0, half, first_half, 0)
-    lax.fori_loop(half, layers, second_half, 0)
     def weight_sq(layer, kind):
         w_copy(layer, kind).wait()
         ref = (wv_in, wv_out)[kind]
@@ -243,13 +244,19 @@
             weight_sq(layer, kind)
         return carry
 
-    lax.fori_loop(0, layers - 1, weights, 0)
-    lax.fori_loop(half, layers, upd_tail, 0)
+    form_layer(0, False, True)
+    spread_old()
+    lax.fori_loop(1, half, first_half, 0)
+    lax.fori_loop(half, layers, second_half, 0)
+    lax.fori_loop(0, 2, weights, 0)
+    lax.fori_loop(2, 3, upd_tail, 0)
+    lax.fori_loop(2, 3, weights, 0)
+    lax.fori_loop(3, 4, upd_tail, 0)
     upd_buf[me] = pack[...]
     for step in range(1, n_dev):
         fin_copy(upd_buf, 0, step).start()
 
-    lax.fori_loop(layers - 1, layers, weights, 0)
+    lax.fori_loop(3, 4, weights, 0)
     wsq_buf[me] = wpack[...]
     for step in range(1, n_dev):
         fin_copy(wsq_buf, 1, step).start()
@@ -392,7 +399,7 @@
                 pltpu.VMEM((ms, LANE), F32), pltpu.VMEM((8, ml), F32),
                 pltpu.VMEM((lch, LANE), F32), pltpu.VMEM((1, LANE), F32), pltpu.VMEM((1, LANE), F32),
                 pltpu.SMEM((3,), F32),
-                dma((4, 2)), dma((layers, 2)), dma((5,)),
+                dma((4, 1 + ml // CHUNK)), dma((layers, 2)), dma((5,)),
                 dma((mats,)), dma((mats,)), dma((mats,)), dma((mats,)), dma((2,)), dma((2,)),
             ],
             compiler_params=pltpu.CompilerParams(

time: 30.7 us -> 30.4 us (level)
  no operation moved by 1% of the time
where the time goes in v5:
time: 30.4 us; the launch traced here: 30.3 us
  Pallas kernels  29.7 us (98%)
  between operations  0.64 us (2%)
    pallas_call x1, Pallas kernels, local_step(): pl.pallas_call(functools.partial(stats_kernel, dims), out_shape=(pltpu.VM...  22.2 us
    pallas_call x1, Pallas kernels, local_step(): pl.pallas_call(functools.partial(write_kernel, (layers, ms, ml, parts)),...  7.45 us

profile of v5, /device:TPU:0, one launch (start us, length us, event | category | flops | bytes accessed | tf_op | source)
XLA Modules:
  0.0 30.3 jit_solution(335712258387019138)
XLA Ops:
  0.6 22.2 %stats.1 = (f32[4,256,2560]{2,1,0:T(8,128)S(1)}, f32[4,256,2560]{2,1,0:T(8,128)S(1)}, f32[4,256,2560]{2,1,0:T(8,128)S(1)}, f32[4,2560,256]{2,1,0:T(8,128)S(1)}, ...) custom-call(f32[3]{0:T(128)} %hyper_hbm.1, ...), custom_call_target="tpu_custom_call" | custom-call | tf_op jit(solution)/shard_map/stats/pallas_call | solution.py:382
  22.9 7.5 %write.1 = (f32[4,256,2560]{2,1,0:T(8,128)}, f32[4,256]{1,0:T(4,128)}, f32[4,2560]{1,0:T(4,128)}, f32[4,2560,256]{2,1,0:T(8,128)}, f32[4,2560]{1,0:T(4,128)}, /*index=5*/f32[4,256]{1,0:T(4,128)}) custom-call(f32[4,256,2560]{2,1,0:T(8,128)S(1)} %get-tuple-element.15.grad_lo, f32[4,256,2560]{2,1,0:T(8,128)S(1)} %get-tuple-element.16.grad_hi, ...), custom_call_target="tpu_custom_call" | custom-call | tf_op jit(solution)/shard_map/write/pallas_call | solution.py:412

commit v6 on v5

--- a/solution.py
+++ b/solution.py
@@ -10,7 +10,7 @@
 EPS_ONE = 1e-30
 EPS_TWO = 1e-3
 LANE = 128
-CHUNK = 1280
+CHUNK = 512
 WSTEPS = 32
 MESH = pl.DeviceIdType.MESH
 F32 = jnp.float32

time: 30.4 us -> 30.7 us (level)
  no operation moved by 1% of the time
where the time goes in v6:
time: 30.7 us; the launch traced here: 30.6 us
  Pallas kernels  30 us (98%)
  between operations  0.64 us (2%)
    pallas_call x1, Pallas kernels, local_step(): pl.pallas_call(functools.partial(stats_kernel, dims), out_shape=(pltpu.VM...  22.5 us
    pallas_call x1, Pallas kernels, local_step(): pl.pallas_call(functools.partial(write_kernel, (layers, ms, ml, parts)),...  7.45 us

profile of v6, /device:TPU:0, one launch (start us, length us, event | category | flops | bytes accessed | tf_op | source)
XLA Modules:
  0.0 30.6 jit_solution(12095081942819842498)
XLA Ops:
  0.6 22.5 %stats.1 = (f32[4,256,2560]{2,1,0:T(8,128)S(1)}, f32[4,256,2560]{2,1,0:T(8,128)S(1)}, f32[4,256,2560]{2,1,0:T(8,128)S(1)}, f32[4,2560,256]{2,1,0:T(8,128)S(1)}, ...) custom-call(f32[3]{0:T(128)} %hyper_hbm.1, ...), custom_call_target="tpu_custom_call" | custom-call | tf_op jit(solution)/shard_map/stats/pallas_call | solution.py:382
  23.2 7.5 %write.1 = (f32[4,256,2560]{2,1,0:T(8,128)}, f32[4,256]{1,0:T(4,128)}, f32[4,2560]{1,0:T(4,128)}, f32[4,2560,256]{2,1,0:T(8,128)}, f32[4,2560]{1,0:T(4,128)}, /*index=5*/f32[4,256]{1,0:T(4,128)}) custom-call(f32[4,256,2560]{2,1,0:T(8,128)S(1)} %get-tuple-element.15.grad_lo, f32[4,256,2560]{2,1,0:T(8,128)S(1)} %get-tuple-element.16.grad_hi, ...), custom_call_target="tpu_custom_call" | custom-call | tf_op jit(solution)/shard_map/write/pallas_call | solution.py:412
